TPU v7x, 128 devices: a whole 4x4x4 slice. The times are simulated.
128 devices in a mesh: dom: 16 (over x, y), sub: 8 (over z, core).
Axes of the slice: x: 4, y: 4, z: 4, core: 2. Of those that a mesh axis runs over, the one named last changes fastest.
Arguments:
- features: bfloat16 [131072, 602], P(('dom', 'sub')), may hold values from -6 to 6
- w_inner: bfloat16 [602, 256], replicated, may hold values from -0.25 to 0.25
- bias_inner: float32 [256], replicated, may hold values from -6 to 6
- w_outer: bfloat16 [256, 41], replicated, may hold values from -0.375 to 0.375
- bias_outer: float32 [41], replicated, may hold values from -6 to 6
- tiles: bfloat16 [1024, 32, 128, 128], P(('dom', 'sub')), may hold values from -3 to 3
- tile_col: int32 [1024, 32], P(('dom', 'sub')), may hold values from 0 to 135, as said below
- degrees: int32 [131072], P(('dom', 'sub')), may hold values from 1 to 32
- send_rows: int32 [128, 128, 128], P(('dom', 'sub')), may hold values from -1 to 1023, as said below
Outputs:
- logits: float32 [131072, 41], P(('dom', 'sub'))
Inputs may be any that keep to these rules, and one draw needn't show every extreme that they name: send_rows[e, p, s] is the row, among device e's 1024 vertices, that fills slot s of e's list for device p, or -1 for an unused slot; live slots come first and every list has 1 to 128 live slots; every sender has a full list, and in every draw some device receives full lists from all senders. tile_col[d * 8 + r, t] is the column block, in device d's column space, of tile t of row block r; the 32 column blocks of a row block are distinct.
All inputs are finite; a program needn't handle non-finite values.
Results may differ from a plain program's by a relative error of at most 0.0042.
Values may be sent and summed in bfloat16 or wider, within the bound.
A program may use at most 128 MiB of HBM per device.

v0:
```python
import jax
import jax.numpy as jnp
from jax import lax
from jax.sharding import PartitionSpec as P


def deliver_inner(outgoing):
    return lax.all_to_all(outgoing, ("dom", "sub"), split_axis=0, concat_axis=0, tiled=True)


def deliver_outer(outgoing):
    return lax.all_to_all(outgoing, ("dom", "sub"), split_axis=0, concat_axis=0, tiled=True)


def aggregate(feature_rows, tiles, tile_col, send_lists, deliver):
    block_rows = tiles.shape[2]
    width = feature_rows.shape[1]
    clipped = jnp.clip(send_lists, 0, feature_rows.shape[0] - 1)
    live_slot = (send_lists >= 0)[:, :, None]
    outgoing = jnp.where(
        live_slot, jnp.take(feature_rows, clipped, axis=0), jnp.zeros((), feature_rows.dtype)
    )
    arrived = deliver(outgoing)
    columns = jnp.concatenate([feature_rows.reshape(-1, block_rows, width), arrived], axis=0)

    def rowblock(element):
        tile_set, col_set = element
        blocks = columns[col_set]
        return jnp.einsum("tij,tjw->iw", tile_set, blocks, preferred_element_type=jnp.float32)

    summed = lax.map(rowblock, (tiles, tile_col))
    return summed.reshape(feature_rows.shape[0], width)


def on_device(
    features, w_inner, bias_inner, w_outer, bias_outer, tiles, tile_col, degrees, send_rows
):
    send_lists = send_rows[0]
    classes = w_outer.shape[1]
    padded_width = 128 * ((classes + 127) // 128)
    inv_sqrt = lax.rsqrt(degrees.astype(jnp.float32))[:, None]
    projected = (jnp.dot(features, w_inner, preferred_element_type=jnp.float32) * inv_sqrt).astype(
        jnp.bfloat16
    )
    agg_inner = aggregate(projected, tiles, tile_col, send_lists, deliver_inner)
    hidden = (inv_sqrt * jax.nn.relu(inv_sqrt * agg_inner + bias_inner)).astype(jnp.bfloat16)
    w_padded = jnp.pad(w_outer, ((0, 0), (0, padded_width - classes)))
    scores = jnp.dot(hidden, w_padded, preferred_element_type=jnp.float32).astype(jnp.bfloat16)
    agg_outer = aggregate(scores, tiles, tile_col, send_lists, deliver_outer)
    return inv_sqrt * agg_outer[:, :classes] + bias_outer


def solution(mesh):
    return jax.shard_map(
        on_device,
        mesh=mesh,
        in_specs=(
            P(("dom", "sub"), None),
            P(),
            P(),
            P(),
            P(),
            P(("dom", "sub"), None, None, None),
            P(("dom", "sub"), None),
            P(("dom", "sub")),
            P(("dom", "sub"), None, None),
        ),
        out_specs=P(("dom", "sub"), None),
        check_vma=False,
    )
```

profile of v0, /device:TPU:1, one launch (start us, length us, event | category | flops | bytes accessed | tf_op | source)
XLA Modules:
  0.0 435.1 jit_solution(853206017263194829)
XLA Ops:
  0.0 1.0 fusion.18
  1.0 0.9 compare_and_fusion
  1.8 0.9 compare_bitcast_fusion
  2.7 0.7 convert_rsqrt_fusion
  3.4 1.6 fusion.12
  5.0 65.3 %gather_fusion.2 = bf16[16384,256]{1,0:T(8,128)(2,1)} fusion(bf16[1024,256]{1,0:T(8,128)(2,1)S(1)} %fusion.12, s32[16384]{0:T(1024)S(1)} %fusion.18), kind=kCustom, calls=%fused_computation.2 | custom fusion | bytes 16842752 | tf_op jit(solution)/shard_map/jit(_take)/gather | solution.py:21
  70.3 7.7 %select_select_fusion = bf16[128,128,256]{2,1,0:T(8,128)(2,1)} fusion(bf16[128,128,256]{2,1,0:T(8,128)(2,1)} %bitcast.87, pred[128,128]{1,0:T(8,128)(4,1)S(1)} %compare_and_fusion, pred[128,128]{1,0:T(8,128)(4,1)S(1)} %compare_bitcast_fusion), kind=kLoop, calls=%fused_computation.25 | loop fusion | flops 8388608 | bytes 16809984 | tf_op jit(solution)/shard_map/jit(_where)/select_n | solution.py:20
  78.0 11.9 %all-to-all-start = ((bf16[128,128,256]{2,1,0:T(8,128)(2,1)}), bf16[128,128,256]{2,1,0:T(8,128)(2,1)}, u32[]{:S(2)}, u32[]{:S(2)}) async-start(bf16[128,128,256]{2,1,0:T(8,128)(2,1)} %select_select_fusion), calls=%async_computation | async-start | bytes 16777216 | tf_op jit(solution)/shard_map/all_to_all | solution.py:8
  89.9 98.9 %all-to-all-done = bf16[128,128,256]{2,1,0:T(8,128)(2,1)} async-done(((bf16[128,128,256]{2,1,0:T(8,128)(2,1)}), bf16[128,128,256]{2,1,0:T(8,128)(2,1)}, u32[]{:S(2)}, u32[]{:S(2)}) %all-to-all-start) | async-done | bytes 8388640 | tf_op jit(solution)/shard_map/all_to_all | solution.py:8
  188.8 7.6 %pad_maximum_fusion = bf16[136,128,256]{2,1,0:T(8,128)(2,1)} fusion(bf16[128,128,256]{2,1,0:T(8,128)(2,1)} %all-to-all-done, bf16[8,128,256]{2,1,0:T(8,128)(2,1)S(1)} %bitcast.85), kind=kLoop, calls=%fused_computation.24 | loop fusion | flops 4456448 | bytes 17825792 | tf_op jit(solution)/shard_map/concatenate | solution.py:24
  196.4 58.0 %while.20 = (s32[]{:T(128)}, f32[8,128,256]{2,1,0:T(8,128)}, bf16[8,32,128,128]{3,2,1,0:T(8,128)(2,1)}, s32[8,32]{1,0:T(8,128)}, bf16[136,128,256]{2,1,0:T(8,128)(2,1)}, /*index=5*/s32[]{:T(128)}) while((s32[]{:T(128)}, f32[8,128,256]{2,1,0:T(8,128)}, bf16[8,32,128,128]{3,2,1,0:T(8,128)(2,1)}, s32[8,32]{1,0:T(8,128)}, ...), condition=%wide.region_1.2_spmd, body=%wide.region_0.1_spmd.sunk | while | flops 268436576 | bytes 7476809 | solution.py:31
  196.4 0.7 fusion.36
  197.1 4.2 gather_fusion
  201.3 2.3 fusion.37
  203.7 0.7 fusion.36
  204.4 4.2 gather_fusion
  208.6 2.3 fusion.37
  210.9 0.7 fusion.36
  211.6 4.2 gather_fusion
  215.8 2.3 fusion.37
  218.2 0.7 fusion.36
  218.9 4.2 gather_fusion
  223.1 2.3 fusion.37
  226.1 4.2 gather_fusion
  230.3 2.3 fusion.37
  233.4 4.2 gather_fusion
  237.6 2.3 fusion.37
  240.6 4.2 gather_fusion
  244.8 2.3 fusion.37
  247.2 0.7 fusion.36
  247.9 4.2 gather_fusion
  252.1 2.3 fusion.37
  254.4 1.4 fusion.16
  256.2 57.8 %gather_fusion.3 = bf16[16384,128]{1,0:T(8,128)(2,1)} fusion(bf16[1024,128]{1,0:T(8,128)(2,1)S(1)} %convolution_convert_fusion, s32[16384]{0:T(1024)S(1)} %fusion.18), kind=kCustom, calls=%fused_computation.3 | custom fusion | bytes 8454144 | tf_op jit(solution)/shard_map/jit(_take)/gather | solution.py:21
  314.0 7.4 %select_select_fusion.1 = bf16[128,128,128]{2,1,0:T(8,128)(2,1)} fusion(bf16[128,128,128]{2,1,0:T(8,128)(2,1)} %bitcast.88, pred[128,128]{1,0:T(8,128)(4,1)S(1)} %compare_and_fusion, pred[128,128]{1,0:T(8,128)(4,1)S(1)} %compare_bitcast_fusion), kind=kLoop, calls=%fused_computation.27 | loop fusion | flops 4194304 | bytes 8421376 | tf_op jit(solution)/shard_map/jit(_where)/select_n | solution.py:20
  321.4 11.9 %all-to-all-start.1 = ((bf16[128,128,128]{2,1,0:T(8,128)(2,1)}), bf16[128,128,128]{2,1,0:T(8,128)(2,1)}, u32[]{:S(2)}, u32[]{:S(2)}) async-start(bf16[128,128,128]{2,1,0:T(8,128)(2,1)} %select_select_fusion.1), calls=%async_computation.1 | async-start | bytes 8388608 | tf_op jit(solution)/shard_map/all_to_all | solution.py:12
  333.3 52.7 %all-to-all-done.1 = bf16[128,128,128]{2,1,0:T(8,128)(2,1)} async-done(((bf16[128,128,128]{2,1,0:T(8,128)(2,1)}), bf16[128,128,128]{2,1,0:T(8,128)(2,1)}, u32[]{:S(2)}, u32[]{:S(2)}) %all-to-all-start.1) | async-done | bytes 4194336 | tf_op jit(solution)/shard_map/all_to_all | solution.py:12
  386.0 4.6 %pad_maximum_fusion.1 = bf16[136,128,128]{2,1,0:T(8,128)(2,1)} fusion(bf16[128,128,128]{2,1,0:T(8,128)(2,1)} %all-to-all-done.1, bf16[8,128,128]{2,1,0:T(8,128)(2,1)S(1)} %bitcast.86), kind=kLoop, calls=%fused_computation.26 | loop fusion | flops 2228224 | bytes 8912896 | tf_op jit(solution)/shard_map/concatenate | solution.py:24
  390.6 43.2 %while.21 = (s32[]{:T(128)}, f32[8,128,128]{2,1,0:T(8,128)S(1)}, bf16[8,32,128,128]{3,2,1,0:T(8,128)(2,1)}, s32[8,32]{1,0:T(8,128)}, bf16[136,128,128]{2,1,0:T(8,128)(2,1)}, /*index=5*/s32[]{:T(128)}) while((s32[]{:T(128)}, f32[8,128,128]{2,1,0:T(8,128)S(1)}, bf16[8,32,128,128]{3,2,1,0:T(8,128)(2,1)}, s32[8,32]{1,0:T(8,128)}, ...), condition=%wide.region_3.4_spmd, body=%wide.region_2.3_spmd.sunk | while | flops 134218848 | bytes 4265545 | solution.py:31
  390.6 0.7 fusion.40
  391.3 3.0 gather_fusion.1
  394.3 1.7 fusion.41
  396.0 0.7 fusion.40
  396.7 3.0 gather_fusion.1
  399.7 1.7 fusion.41
  401.4 0.7 fusion.40
  402.1 3.0 gather_fusion.1
  405.1 1.7 fusion.41
  406.8 0.7 fusion.40
  407.5 3.0 gather_fusion.1
  410.5 1.7 fusion.41
  412.2 0.7 fusion.40
  412.9 3.0 gather_fusion.1
  415.9 1.7 fusion.41
  417.5 0.7 fusion.40
  418.3 3.0 gather_fusion.1
  421.3 1.7 fusion.41
  422.9 0.7 fusion.40
  423.6 3.0 gather_fusion.1
  426.7 1.7 fusion.41
  428.3 0.7 fusion.40
  429.0 3.0 gather_fusion.1
  432.1 1.7 fusion.41
  433.9 0.8 multiply_add_fusion
  (33 shorter events, 3.1 us)
Async XLA Ops:
  0.0 3.4 copy-start
  78.0 110.8 %all-to-all-start = ((bf16[128,128,256]{2,1,0:T(8,128)(2,1)}), bf16[128,128,256]{2,1,0:T(8,128)(2,1)}, u32[]{:S(2)}, u32[]{:S(2)}) async-start(bf16[128,128,256]{2,1,0:T(8,128)(2,1)} %select_select_fusion), calls=%async_computation | async-start | bytes 16777216 | tf_op jit(solution)/shard_map/all_to_all | solution.py:8
  196.4 58.0 %copy-start.3 = (f32[256]{0:T(256)S(1)}, f32[256]{0:T(256)}, u32[]{:S(2)}) copy-start(f32[256]{0:T(256)} %param.15) | copy-start | bytes 3076
  196.4 59.5 %copy-start.2 = (bf16[256,41]{0,1:T(8,128)(2,1)S(1)}, bf16[256,41]{0,1:T(8,128)(2,1)}, u32[]{:S(2)}) copy-start(bf16[256,41]{0,1:T(8,128)(2,1)} %param.16) | copy-start | bytes 62980
  321.4 64.6 %all-to-all-start.1 = ((bf16[128,128,128]{2,1,0:T(8,128)(2,1)}), bf16[128,128,128]{2,1,0:T(8,128)(2,1)}, u32[]{:S(2)}, u32[]{:S(2)}) async-start(bf16[128,128,128]{2,1,0:T(8,128)(2,1)} %select_select_fusion.1), calls=%async_computation.1 | async-start | bytes 8388608 | tf_op jit(solution)/shard_map/all_to_all | solution.py:12
  390.6 43.4 %copy-start.4 = (f32[41]{0:T(128)S(1)}, f32[41]{0:T(128)}, u32[]{:S(2)}) copy-start(f32[41]{0:T(128)} %param.17) | copy-start | bytes 496
  433.7 1.4 copy-start.1
where the time goes:
time: 437 us; the launch traced here: 435 us
  local copies, waits for them, and re-layouts  181 us (41%)
  waiting for transfers between devices  152 us (35%)
  other arithmetic  44.1 us (10%)
  matrix products  33.7 us (8%)
  starting transfers between devices  23.8 us (5%)
    gather x2, local copies, waits for them, and re-layouts, aggregate(): jnp.take(feature_rows, clipped, axis=0)  123 us
    all_to_all x1, waiting for transfers between devices, deliver_inner(): lax.all_to_all(outgoing, ('dom', 'sub'), split_axis=0, concat_axis=0, til...  98.9 us
    gather x16, local copies, waits for them, and re-layouts, rowblock(): blocks = columns[col_set]  57.8 us
    all_to_all x1, waiting for transfers between devices, deliver_outer(): lax.all_to_all(outgoing, ('dom', 'sub'), split_axis=0, concat_axis=0, til...  52.7 us
    dot_general x16, matrix products, rowblock(): jnp.einsum('tij,tjw->iw', tile_set, blocks, preferred_element_type=jnp.fl...  31.8 us
    select_n x2, other arithmetic, aggregate(): jnp.where(live_slot, jnp.take(feature_rows, clipped, axis=0), jnp.zeros((...  15.1 us
    concatenate x2, other arithmetic, aggregate(): jnp.concatenate([feature_rows.reshape(-1, block_rows, width), arrived], a...  12.2 us
    all_to_all x1, starting transfers between devices, deliver_inner(): lax.all_to_all(outgoing, ('dom', 'sub'), split_axis=0, concat_axis=0, til...  11.9 us
  transfers between devices with their start and end apart: 2, of which 2 were waited for; matrix products, arithmetic and copies ran while one was open for 0% of the time, Pallas kernels for 0%

commit v1 on v0

v1 whole, which is shorter than its diff:
```python
import functools

import jax
import jax.numpy as jnp
from jax import lax
from jax.experimental import pallas as pl
from jax.experimental.pallas import tpu as pltpu
from jax.sharding import PartitionSpec as P

BLOCK = 128
CHUNK = 256
LISTS = 8


def pick_rows(stacked, lists, width):
    parts = stacked.shape[0] // width
    index = jnp.concatenate([lists[0:1], lists[1:2]], axis=1)
    low = jnp.where(index >= 0, lax.rem(index, CHUNK), -1)
    high = lax.shift_right_arithmetic(index, 8)
    lane = lax.broadcasted_iota(jnp.int32, (CHUNK, 2 * BLOCK), 0)
    onehot = jnp.where(lane == low, 1.0, 0.0).astype(jnp.bfloat16)
    found = jnp.dot(stacked, onehot, preferred_element_type=jnp.float32)
    total = jnp.zeros((width, 2 * BLOCK), jnp.float32)
    for part in range(parts):
        total = jnp.where(high == part, found[part * width : (part + 1) * width], total)
    return total.astype(jnp.bfloat16)


def fill_lists(stacked, send_ref, out_ref, width):
    for pair in range(LISTS // 2):
        picked = pick_rows(stacked[...], send_ref[2 * pair : 2 * pair + 2, :], width)
        out_ref[2 * pair] = picked[:, :BLOCK]
        out_ref[2 * pair + 1] = picked[:, BLOCK:]


def project_kernel(features, w_inner, degrees, send, lists, local, stacked):
    width = w_inner.shape[1]

    @pl.when(pl.program_id(0) == 0)
    def _():
        inv_sqrt = lax.rsqrt(degrees[...].astype(jnp.float32))
        for part in range(stacked.shape[0] // width):
            rows = slice(part * CHUNK, (part + 1) * CHUNK)
            product = lax.dot_general(
                w_inner[...],
                features[rows, :],
                (((0,), (1,)), ((), ())),
                preferred_element_type=jnp.float32,
            )
            piece = (product * inv_sqrt[:, rows]).astype(jnp.bfloat16)
            stacked[part * width : (part + 1) * width, :] = piece
            local[2 * part] = piece[:, :BLOCK]
            local[2 * part + 1] = piece[:, BLOCK:]

    fill_lists(stacked, send, lists, width)


def gather_kernel(scores, send, lists, stacked):
    width = scores.shape[1]

    @pl.when(pl.program_id(0) == 0)
    def _():
        for block in range(scores.shape[0]):
            part, half = block // 2, block % 2
            stacked[part * width : (part + 1) * width, half * BLOCK : (half + 1) * BLOCK] = scores[block]

    fill_lists(stacked, send, lists, width)


def summed(tile_col, tiles, columns, row):
    total = None
    for pair in range(tiles.shape[1] // 2):
        first, second = tile_col[row, 2 * pair], tile_col[row, 2 * pair + 1]
        rows = jnp.concatenate([columns[first], columns[second]], axis=1)
        edges = jnp.concatenate([tiles[0, 2 * pair], tiles[0, 2 * pair + 1]], axis=1)
        product = lax.dot_general(
            rows, edges, (((1,), (1,)), ((), ())), preferred_element_type=jnp.float32
        )
        total = product if total is None else total + product
    return total


def load_columns(local, arrived, columns, sems):
    @pl.when(pl.program_id(0) == 0)
    def _():
        own = local.shape[0]
        first = pltpu.make_async_copy(local, columns.at[pl.ds(0, own)], sems.at[0])
        second = pltpu.make_async_copy(arrived, columns.at[pl.ds(own, arrived.shape[0])], sems.at[1])
        first.start()
        second.start()
        first.wait()
        second.wait()


def inner_kernel(tile_col, tiles, local, arrived, degrees, bias, w_outer, scores, columns, sems):
    load_columns(local, arrived, columns, sems)
    inv_sqrt = lax.rsqrt(degrees[...].astype(jnp.float32))
    aggregated = summed(tile_col, tiles, columns, pl.program_id(0))
    hidden = inv_sqrt * jnp.maximum(inv_sqrt * aggregated + bias[...], 0.0)
    result = jnp.dot(w_outer[...], hidden.astype(jnp.bfloat16), preferred_element_type=jnp.float32)
    scores[0] = result.astype(jnp.bfloat16)


def outer_kernel(tile_col, tiles, local, arrived, degrees, bias, logits, columns, sems):
    load_columns(local, arrived, columns, sems)
    inv_sqrt = lax.rsqrt(degrees[...].astype(jnp.float32))
    aggregated = summed(tile_col, tiles, columns, pl.program_id(0))
    result = inv_sqrt * aggregated + bias[...]
    logits[...] = jnp.transpose(result)[:, : logits.shape[1]]


VMEM_LIMIT = 60 * 1024 * 1024


def whole(shape):
    return pl.BlockSpec(shape, lambda step: (0,) * len(shape))


def params():
    return pltpu.CompilerParams(
        dimension_semantics=("arbitrary",), vmem_limit_bytes=VMEM_LIMIT
    )


def on_device(features, w_inner, bias_inner, w_outer, bias_outer, tiles, tile_col, degrees, send_rows):
    send = send_rows[0]
    rows, depth = features.shape
    hidden = w_inner.shape[1]
    classes = w_outer.shape[1]
    padded = 16 * ((classes + 15) // 16)
    peers = send.shape[0]
    blocks, per_block = tile_col.shape
    degrees = degrees.reshape(1, rows)
    parts = rows // CHUNK

    lists, local = pl.pallas_call(
        project_kernel,
        grid=(peers // LISTS,),
        out_shape=(
            jax.ShapeDtypeStruct((peers, hidden, BLOCK), jnp.bfloat16),
            jax.ShapeDtypeStruct((blocks, hidden, BLOCK), jnp.bfloat16),
        ),
        in_specs=[
            whole((rows, depth)),
            whole((depth, hidden)),
            whole((1, rows)),
            pl.BlockSpec((LISTS, BLOCK), lambda step: (step, 0)),
        ],
        out_specs=(
            pl.BlockSpec((LISTS, hidden, BLOCK), lambda step: (step, 0, 0)),
            whole((blocks, hidden, BLOCK)),
        ),
        scratch_shapes=[pltpu.VMEM((parts * hidden, CHUNK), jnp.bfloat16)],
        compiler_params=params(),
    )(features, w_inner, degrees, send)

    def aggregate(body, local, arrived, extras, extra_specs, out_shape, out_spec):
        width = local.shape[1]
        return pl.pallas_call(
            body,
            grid=(blocks,),
            out_shape=out_shape,
            in_specs=[
                pl.BlockSpec(memory_space=pltpu.SMEM),
                pl.BlockSpec((1, per_block, BLOCK, BLOCK), lambda step: (step, 0, 0, 0)),
                pl.BlockSpec(memory_space=pl.ANY),
                pl.BlockSpec(memory_space=pl.ANY),
                pl.BlockSpec((1, BLOCK), lambda step: (0, step)),
            ]
            + extra_specs,
            out_specs=out_spec,
            scratch_shapes=[
                pltpu.VMEM((blocks + peers, width, BLOCK), jnp.bfloat16),
                pltpu.SemaphoreType.DMA((2,)),
            ],
            compiler_params=params(),
        )(tile_col, tiles, local, arrived, degrees, *extras)

    arrived = lax.all_to_all(lists, ("dom", "sub"), split_axis=0, concat_axis=0, tiled=True)
    w_padded = jnp.pad(w_outer.T, ((0, padded - classes), (0, 0)))
    scores = aggregate(
        inner_kernel,
        local,
        arrived,
        (bias_inner.reshape(hidden, 1), w_padded),
        [whole((hidden, 1)), whole((padded, hidden))],
        jax.ShapeDtypeStruct((blocks, padded, BLOCK), jnp.bfloat16),
        pl.BlockSpec((1, padded, BLOCK), lambda step: (step, 0, 0)),
    )

    lists = pl.pallas_call(
        gather_kernel,
        grid=(peers // LISTS,),
        out_shape=jax.ShapeDtypeStruct((peers, padded, BLOCK), jnp.bfloat16),
        in_specs=[
            whole((blocks, padded, BLOCK)),
            pl.BlockSpec((LISTS, BLOCK), lambda step: (step, 0)),
        ],
        out_specs=pl.BlockSpec((LISTS, padded, BLOCK), lambda step: (step, 0, 0)),
        scratch_shapes=[pltpu.VMEM((parts * padded, CHUNK), jnp.bfloat16)],
        compiler_params=params(),
    )(scores, send)

    arrived = lax.all_to_all(lists, ("dom", "sub"), split_axis=0, concat_axis=0, tiled=True)
    bias_padded = jnp.pad(bias_outer, (0, padded - classes)).reshape(padded, 1)
    return aggregate(
        outer_kernel,
        scores,
        arrived,
        (bias_padded,),
        [whole((padded, 1))],
        jax.ShapeDtypeStruct((rows, classes), jnp.float32),
        pl.BlockSpec((BLOCK, classes), lambda step: (step, 0)),
    )


def solution(mesh):
    return jax.shard_map(
        on_device,
        mesh=mesh,
        in_specs=(
            P(("dom", "sub"), None),
            P(),
            P(),
            P(),
            P(),
            P(("dom", "sub"), None, None, None),
            P(("dom", "sub"), None),
            P(("dom", "sub")),
            P(("dom", "sub"), None, None),
        ),
        out_specs=P(("dom", "sub"), None),
        check_vma=False,
    )
```

time: 437 us -> 203 us (0.46)
  local copies, waits for them, and re-layouts: 181 us -> 7.61 us
  Pallas kernels: 0 us -> 49.3 us
  other arithmetic: 44.1 us -> 0 us
  matrix products: 33.7 us -> 0 us
  waiting for transfers between devices: 152 us -> 122 us
    gather x18 -> x0, local copies, waits for them, and re-layouts: 181 us -> none  [the longest x2 123 us: aggregate(): jnp.take(feature_rows, clipped, axis=0)]
    pallas_call x0 -> x4, Pallas kernels: none -> 49.3 us  [the longest x2 24.1 us: aggregate(): pl.pallas_call(body, grid=(blocks,), out_shape=out_shape, in_specs=[pl.Bl...]
    dot_general x18 -> x0, matrix products: 33.7 us -> none  [the longest x16 31.8 us: rowblock(): jnp.einsum('tij,tjw->iw', tile_set, blocks, preferred_element_type=jnp.fl...]
    all_to_all x2, waiting for transfers between devices: 152 us -> 122 us  [on_device(): lax.all_to_all(lists, ('dom', 'sub'), split_axis=0, concat_axis=0, tiled=...]
    select_n x18 -> x0, other arithmetic: 26.2 us -> none  [the longest x2 15.1 us: aggregate(): jnp.where(live_slot, jnp.take(feature_rows, clipped, axis=0), jnp.zeros((...]
    concatenate x2 -> x0, other arithmetic: 12.2 us -> none  [aggregate(): jnp.concatenate([feature_rows.reshape(-1, block_rows, width), arrived], a...]
  transfers between devices with their start and end apart: 2 -> 2, of which waited for: 2 -> 2; matrix products, arithmetic and copies ran while one was open for 0% -> 1% of each run, Pallas kernels for 0% -> 0%
where the time goes in v1:
time: 203 us; the launch traced here: 202 us
  waiting for transfers between devices  122 us (60%)
  Pallas kernels  49.3 us (24%)
  starting transfers between devices  23.3 us (11%)
  local copies, waits for them, and re-layouts  7.61 us (4%)
    all_to_all x2, waiting for transfers between devices, on_device(): lax.all_to_all(lists, ('dom', 'sub'), split_axis=0, concat_axis=0, tiled=...  122 us
    pallas_call x2, Pallas kernels, aggregate(): pl.pallas_call(body, grid=(blocks,), out_shape=out_shape, in_specs=[pl.Bl...  24.1 us
    all_to_all x2, starting transfers between devices, on_device(): lax.all_to_all(lists, ('dom', 'sub'), split_axis=0, concat_axis=0, tiled=...  23.3 us
    pallas_call x1, Pallas kernels, on_device(): pl.pallas_call(project_kernel, grid=(peers // LISTS,), out_shape=(jax.Sha...  15.4 us
    pallas_call x1, Pallas kernels, on_device(): pl.pallas_call(gather_kernel, grid=(peers // LISTS,), out_shape=jax.Shape...  9.85 us
  transfers between devices with their start and end apart: 2, of which 2 were waited for; matrix products, arithmetic and copies ran while one was open for 1% of the time, Pallas kernels for 0%

profile of v1, /device:TPU:1, one launch (start us, length us, event | category | flops | bytes accessed | tf_op | source)
XLA Modules:
  0.0 201.8 jit_solution(13068751180580239826)
XLA Ops:
  0.0 2.4 %copy.13.features = bf16[1024,602]{1,0:T(8,128)(2,1)} copy(bf16[1024,602]{0,1:T(8,128)(2,1)} %param.9) | data formatting | bytes 2465792 | tf_op args[0]
  2.4 15.4 %shard_map.91 = (bf16[128,256,128]{2,1,0:T(8,128)(2,1)}, bf16[8,256,128]{2,1,0:T(8,128)(2,1)}) custom-call(bf16[1024,602]{1,0:T(8,128)(2,1)} %copy.13.features, bf16[602,256]{1,0:T(8,128)(2,1)} %w_inner.1, s32[1,1024]{1,0:T(1,128)} %bitcast.8, s32[128,128]{1,0:T(8,128)} %bitcast.6), custom_call_target="tpu_custom_call" | custom-call | tf_op jit(solution)/shard_map/pallas_call | solution.py:136
  17.8 0.0 copy-start.2
  17.8 0.0 copy-start.1
  17.8 11.9 %all-to-all-start = ((bf16[128,256,128]{2,1,0:T(8,128)(2,1)}), bf16[128,256,128]{2,1,0:T(8,128)(2,1)}, u32[]{:S(2)}, u32[]{:S(2)}) async-start(bf16[128,256,128]{2,1,0:T(8,128)(2,1)} %get-tuple-element.8), calls=%async_computation | async-start | bytes 16777216 | tf_op jit(solution)/shard_map/all_to_all | solution.py:179
  29.8 0.0 copy-done.2
  29.8 0.8 copy.14.bias
  30.6 0.0 copy-done.1
  30.6 0.6 pad.8.w_outer
  31.2 97.5 %all-to-all-done.arrived = bf16[128,256,128]{2,1,0:T(8,128)(2,1)} async-done(((bf16[128,256,128]{2,1,0:T(8,128)(2,1)}), bf16[128,256,128]{2,1,0:T(8,128)(2,1)}, u32[]{:S(2)}, u32[]{:S(2)}) %all-to-all-start) | async-done | bytes 8388640 | tf_op jit(solution)/shard_map/all_to_all | solution.py:179
  128.7 13.8 %shard_map.92.scores.local = bf16[8,48,128]{2,1,0:T(8,128)(2,1)} custom-call(s32[8,32]{1,0:T(8,128)} %tile_col.3, bf16[8,32,128,128]{3,2,1,0:T(8,128)(2,1)} %tiles.3, bf16[8,256,128]{2,1,0:T(8,128)(2,1)} %get-tuple-element.7.local, bf16[128,256,128]{2,1,0:T(8,128)(2,1)} %all-to-all-done.arrived, s32[1,1024]{1,0:T(1,128)} %bitcast.9, f32[256,1]{1,0:T(8,128)} %copy.14.bias, ...), custom_call_target="tpu_custom_call" | custom-call | tf_op jit(solution)/shard_map/pallas_call | solution.py:159
  142.4 9.9 %shard_map.93 = bf16[128,48,128]{2,1,0:T(8,128)(2,1)} custom-call(bf16[8,48,128]{2,1,0:T(8,128)(2,1)} %shard_map.92.scores.local, s32[128,128]{1,0:T(8,128)} %bitcast.7), custom_call_target="tpu_custom_call" | custom-call | tf_op jit(solution)/shard_map/pallas_call | solution.py:191
  152.3 0.0 copy-start.3
  152.3 11.4 %all-to-all-start.1 = ((bf16[128,48,128]{2,1,0:T(8,128)(2,1)}), bf16[128,48,128]{2,1,0:T(8,128)(2,1)S(1)}, u32[]{:S(2)}, u32[]{:S(2)}) async-start(bf16[128,48,128]{2,1,0:T(8,128)(2,1)} %shard_map.93), calls=%async_computation.1 | async-start | bytes 3145728 | tf_op jit(solution)/shard_map/all_to_all | solution.py:204
  163.7 0.0 copy-done.3
  163.7 0.7 copy.15.bias
  164.4 24.1 %all-to-all-done.1.arrived = bf16[128,48,128]{2,1,0:T(8,128)(2,1)S(1)} async-done(((bf16[128,48,128]{2,1,0:T(8,128)(2,1)}), bf16[128,48,128]{2,1,0:T(8,128)(2,1)S(1)}, u32[]{:S(2)}, u32[]{:S(2)}) %all-to-all-start.1) | async-done | bytes 1572896 | tf_op jit(solution)/shard_map/all_to_all | solution.py:204
  188.5 0.0 copy-start
  188.5 1.1 copy-done
  189.6 10.3 %shard_map.94 = f32[1024,41]{1,0:T(8,128)} custom-call(s32[8,32]{1,0:T(8,128)} %tile_col.3, bf16[8,32,128,128]{3,2,1,0:T(8,128)(2,1)} %tiles.3, bf16[8,48,128]{2,1,0:T(8,128)(2,1)} %shard_map.92.scores.local, bf16[128,48,128]{2,1,0:T(8,128)(2,1)} %copy-done, s32[1,1024]{1,0:T(1,128)} %bitcast.10, f32[48,1]{1,0:T(8,128)} %copy.15.bias), custom_call_target="tpu_custom_call" | custom-call | tf_op jit(solution)/shard_map/pallas_call | solution.py:159
  199.9 1.9 copy.16
  (1 shorter events, 0.0 us)
Async XLA Ops:
  17.8 12.0 %copy-start.2 = (f32[256]{0:T(256)S(1)}, f32[256]{0:T(256)}, u32[]{:S(2)}) copy-start(f32[256]{0:T(256)} %param.11) | copy-start | bytes 3076
  17.8 12.8 %copy-start.1 = (bf16[256,41]{0,1:T(8,128)(2,1)S(1)}, bf16[256,41]{0,1:T(8,128)(2,1)}, u32[]{:S(2)}) copy-start(bf16[256,41]{0,1:T(8,128)(2,1)} %param.12) | copy-start | bytes 62980
  17.8 110.9 %all-to-all-start = ((bf16[128,256,128]{2,1,0:T(8,128)(2,1)}), bf16[128,256,128]{2,1,0:T(8,128)(2,1)}, u32[]{:S(2)}, u32[]{:S(2)}) async-start(bf16[128,256,128]{2,1,0:T(8,128)(2,1)} %get-tuple-element.8), calls=%async_computation | async-start | bytes 16777216 | tf_op jit(solution)/shard_map/all_to_all | solution.py:179
  152.3 11.4 %copy-start.3 = (f32[41]{0:T(128)S(1)}, f32[41]{0:T(128)}, u32[]{:S(2)}) copy-start(f32[41]{0:T(128)} %param.13) | copy-start | bytes 496
  152.3 36.2 %all-to-all-start.1 = ((bf16[128,48,128]{2,1,0:T(8,128)(2,1)}), bf16[128,48,128]{2,1,0:T(8,128)(2,1)S(1)}, u32[]{:S(2)}, u32[]{:S(2)}) async-start(bf16[128,48,128]{2,1,0:T(8,128)(2,1)} %shard_map.93), calls=%async_computation.1 | async-start | bytes 3145728 | tf_op jit(solution)/shard_map/all_to_all | solution.py:204
  188.5 1.1 copy-start

commit v2 on v0

v2 whole, which is shorter than its diff:
```python
import functools

import jax
import jax.numpy as jnp
from jax import lax
from jax.experimental import pallas as pl
from jax.experimental.pallas import tpu as pltpu
from jax.sharding import PartitionSpec as P

BLOCK = 128
CHUNK = 256
SIDE = 4
CORES = 2
AXES = 3
CHIPS = SIDE * SIDE
PLANE = CHIPS * CORES
MESH = pl.DeviceIdType.MESH
VMEM_LIMIT = 60 * 1024 * 1024


def pick_rows(stacked, lists, width):
    parts = stacked.shape[0] // width
    index = jnp.concatenate([lists[0:1], lists[1:2]], axis=1)
    low = index & (CHUNK - 1)
    high = lax.shift_right_arithmetic(index, 8)
    lane = lax.broadcasted_iota(jnp.int32, (CHUNK, 2 * BLOCK), 0)
    onehot = jnp.where(lane == low, 1.0, 0.0).astype(jnp.bfloat16)
    found = jnp.dot(stacked, onehot, preferred_element_type=jnp.float32)
    total = jnp.zeros((width, 2 * BLOCK), jnp.float32)
    for part in range(parts):
        total = jnp.where(high == part, found[part * width : (part + 1) * width], total)
    return total.astype(jnp.bfloat16)


class Place:
    def __init__(self):
        dom, sub = lax.axis_index("dom"), lax.axis_index("sub")
        self.at = (dom // SIDE, dom % SIDE, sub // CORES)
        self.core = sub % CORES

    def line(self, f):
        return self.at[f]

    def plane(self, f):
        return [self.at[k] for k in range(AXES) if k != f]

    def device(self, f, a, i, j, core):
        spot = [i, j]
        spot.insert(f, a)
        return (spot[0] * SIDE + spot[1], spot[2] * CORES + core)


def chips(f, a, i, j):
    spot = [i, j]
    spot.insert(f, a)
    return tuple(spot)


class Exchange:
    def __init__(self, place, sizes, held, lists, staged, columns, sems):
        self.place, self.sizes, self.held, self.lists = place, sizes, held, lists
        self.staged, self.columns = staged, columns
        self.line_sent, self.line_got, self.sent, self.got = sems
        self.starts = [sum(sizes[:f]) for f in range(AXES)]

    def along_line(self, f, step):
        p = self.place
        a = p.line(f)
        i, j = p.plane(f)
        return pltpu.make_async_remote_copy(
            src_ref=self.held[f].at[a],
            dst_ref=self.held[f].at[a],
            send_sem=self.line_sent.at[f, step - 1],
            recv_sem=self.line_got.at[f, step - 1],
            device_id=p.device(f, (a + step) % SIDE, i, j, p.core),
            device_id_type=MESH,
        )

    def across(self, f, spot, core):
        p = self.place
        i, j = p.plane(f)
        target = ((i + spot // SIDE) % SIDE, (j + spot % SIDE) % SIDE)
        there = self.columns.at[
            chips(f, pl.ds(0, SIDE), i, j)
            + (p.core, pl.ds(self.starts[f], self.sizes[f]), slice(None))
        ]
        return pltpu.make_async_remote_copy(
            src_ref=self.staged[f].at[spot * CORES + core],
            dst_ref=there,
            send_sem=self.sent.at[f, spot * CORES + core],
            recv_sem=self.got.at[f, spot * CORES + p.core],
            device_id=p.device(f, p.line(f), target[0], target[1], core),
            device_id_type=MESH,
        )

    def arrival(self, f, spot, core):
        p = self.place
        i, j = p.plane(f)
        there = self.columns.at[
            chips(f, pl.ds(0, SIDE), i, j)
            + (p.core, pl.ds(self.starts[f], self.sizes[f]), slice(None))
        ]
        return pltpu.make_async_remote_copy(
            src_ref=self.staged[f].at[spot * CORES],
            dst_ref=there,
            send_sem=self.sent.at[f, spot * CORES],
            recv_sem=self.got.at[f, spot * CORES + core],
            device_id=p.device(f, p.line(f), i, j, 1 - p.core),
            device_id_type=MESH,
        )

    def start_lines(self):
        for f in range(AXES):
            for step in range(1, SIDE):
                self.along_line(f, step).start()

    def wait_lines(self):
        for f in range(AXES):
            for step in range(1, SIDE):
                self.along_line(f, step).wait()

    def run_planes(self):
        p = self.place

        @pl.loop(0, CHIPS)
        def _(turn):
            spot = (turn + 1) % CHIPS
            for f in range(AXES):
                i, j = p.plane(f)
                i, j = (i + spot // SIDE) % SIDE, (j + spot % SIDE) % SIDE
                for a in range(SIDE):
                    picked = pick_rows(self.held[f][a], self.lists[f, a, i, j], self.sizes[f])
                    self.staged[f][spot * CORES, a] = picked[:, :BLOCK]
                    self.staged[f][spot * CORES + 1, a] = picked[:, BLOCK:]
                for core in range(CORES):

                    @pl.when(jnp.logical_or(spot != 0, p.core != core))
                    def _():
                        self.across(f, spot, core).start()

        for f in range(AXES):
            i, j = p.plane(f)
            for a in range(SIDE):
                x, y, z = chips(f, a, i, j)
                rows = pl.ds(self.starts[f], self.sizes[f])
                self.columns[x, y, z, p.core, rows, :] = self.staged[f][p.core, a]

        @pl.loop(0, CHIPS)
        def _(spot):
            for f in range(AXES):
                for core in range(CORES):

                    @pl.when(jnp.logical_or(spot != 0, p.core != core))
                    def _():
                        self.across(f, spot, core).wait_send()
                        self.arrival(f, spot, core).wait_recv()


def summed(tile_col, tiles, columns, row):
    total = None

    def column(t):
        c = (tile_col[row, t] + SIDE * PLANE) % (SIDE * PLANE + 8)
        return columns[c // PLANE, (c // 8) % SIDE, (c // CORES) % SIDE, c % CORES]

    for pair in range(tiles.shape[1] // 2):
        rows = jnp.concatenate([column(2 * pair), column(2 * pair + 1)], axis=1)
        edges = jnp.concatenate([tiles[row, 2 * pair], tiles[row, 2 * pair + 1]], axis=1)
        product = lax.dot_general(
            rows, edges, (((1,), (1,)), ((), ())), preferred_element_type=jnp.float32
        )
        total = product if total is None else total + product
    return total


def kernel(sizes_in, sizes_out, *refs):
    (features, w_inner, bias_inner, w_outer, bias_outer, tiles_far, tile_col, degrees, send) = refs[:9]
    logits = refs[9]
    scratch = list(refs[10:])
    tiles, tiles_sem, lists, list_sent, list_got = scratch[:5]
    held_in, staged_in = scratch[5:8], scratch[8:11]
    held_out, staged_out = scratch[11:14], scratch[14:17]
    columns_in, columns_out = scratch[17:19]
    sems_in, sems_out = scratch[19:23], scratch[23:27]

    place = Place()
    load = pltpu.make_async_copy(tiles_far, tiles, tiles_sem)
    load.start()

    barrier = pltpu.get_barrier_semaphore()

    @pl.loop(0, CHIPS)
    def _(spot):
        for f in range(AXES):
            i, j = place.plane(f)
            i, j = (i + spot // SIDE) % SIDE, (j + spot % SIDE) % SIDE
            for core in range(CORES):

                @pl.when(jnp.logical_or(spot != 0, place.core != core))
                def _():
                    pl.semaphore_signal(
                        barrier,
                        inc=1,
                        device_id=place.device(f, place.line(f), i, j, core),
                        device_id_type=MESH,
                    )

    pl.semaphore_wait(barrier, AXES * (PLANE - 1))

    def lists_along(f, step):
        a = place.line(f)
        there = (a + step) % SIDE
        i, j = place.plane(f)
        cut = [slice(None), slice(None)]
        cut.insert(f, there)
        return pltpu.make_async_remote_copy(
            src_ref=send.at[tuple(cut)],
            dst_ref=lists.at[f, a],
            send_sem=list_sent.at[f, step - 1],
            recv_sem=list_got.at[f, step - 1],
            device_id=place.device(f, there, i, j, place.core),
            device_id_type=MESH,
        )

    for f in range(AXES):
        for step in range(1, SIDE):
            lists_along(f, step).start()

    inner = Exchange(place, sizes_in, held_in, lists, staged_in, columns_in, sems_in)
    outer = Exchange(place, sizes_out, held_out, lists, staged_out, columns_out, sems_out)

    def keep(exchange, part, piece):
        for f in range(AXES):
            size = exchange.sizes[f]
            rows = piece[exchange.starts[f] : exchange.starts[f] + size]
            exchange.held[f][place.line(f), pl.ds(part * size, size), :] = rows
        exchange.columns[SIDE, 0, part, 0] = piece[:, :BLOCK]
        exchange.columns[SIDE, 0, part, 1] = piece[:, BLOCK:]

    def scale(part):
        return lax.rsqrt(degrees[:, pl.ds(part * CHUNK, CHUNK)].astype(jnp.float32))

    for part in range(SIDE):
        product = lax.dot_general(
            w_inner[...],
            features[:, part * CHUNK : (part + 1) * CHUNK],
            (((0,), (0,)), ((), ())),
            preferred_element_type=jnp.float32,
        )
        keep(inner, part, (product * scale(part)).astype(jnp.bfloat16))

    inner.start_lines()
    for f in range(AXES):
        a = place.line(f)
        if f == 0:
            lists[f, a] = send[a]
        elif f == 1:
            lists[f, a] = send[:, a]
        else:
            lists[f, a] = send[:, :, a]
    for f in range(AXES):
        for step in range(1, SIDE):
            lists_along(f, step).wait()
    inner.wait_lines()
    inner.run_planes()

    load.wait()

    @pl.loop(0, SIDE)
    def _(part):
        inv_sqrt = scale(part)
        aggregated = jnp.concatenate(
            [summed(tile_col, tiles, columns_in, 2 * part + half) for half in range(2)], axis=1
        )
        hidden = inv_sqrt * jnp.maximum(inv_sqrt * aggregated + bias_inner[...], 0.0)
        result = jnp.dot(w_outer[...], hidden.astype(jnp.bfloat16), preferred_element_type=jnp.float32)
        keep(outer, part, result.astype(jnp.bfloat16))

    outer.start_lines()
    outer.wait_lines()
    outer.run_planes()

    @pl.loop(0, SIDE)
    def _(part):
        aggregated = jnp.concatenate(
            [summed(tile_col, tiles, columns_out, 2 * part + half) for half in range(2)], axis=1
        )
        result = scale(part) * aggregated + bias_outer[...]
        logits[:, pl.ds(part * CHUNK, CHUNK)] = result[: logits.shape[0]]


def on_device(features, w_inner, bias_inner, w_outer, bias_outer, tiles, tile_col, degrees, send_rows):
    rows, _ = features.shape
    hidden = w_inner.shape[1]
    classes = w_outer.shape[1]
    padded = 16 * AXES
    sizes_in, sizes_out = (96, 80, 80), (16, 16, 16)
    send = send_rows.reshape(SIDE, SIDE, SIDE, CORES, BLOCK)
    vmem = pl.BlockSpec(memory_space=pltpu.VMEM)
    bf16 = jnp.bfloat16

    def held(sizes):
        return [pltpu.VMEM((SIDE, SIDE * size, CHUNK), bf16) for size in sizes]

    def staged(sizes):
        return [pltpu.VMEM((PLANE, SIDE, size, BLOCK), bf16) for size in sizes]

    def columns(sizes):
        return pltpu.VMEM((SIDE + 1, SIDE, SIDE, CORES, sum(sizes), BLOCK), bf16)

    def sems():
        few, many = pltpu.SemaphoreType.DMA((AXES, SIDE - 1)), pltpu.SemaphoreType.DMA((AXES, PLANE))
        return [few, few, many, many]

    return pl.pallas_call(
        functools.partial(kernel, sizes_in, sizes_out),
        out_shape=jax.ShapeDtypeStruct((classes, rows), jnp.float32),
        in_specs=[
            vmem,
            vmem,
            vmem,
            vmem,
            vmem,
            pl.BlockSpec(memory_space=pl.ANY),
            pl.BlockSpec(memory_space=pltpu.SMEM),
            vmem,
            vmem,
        ],
        out_specs=vmem,
        scratch_shapes=[
            pltpu.VMEM(tiles.shape, bf16),
            pltpu.SemaphoreType.DMA,
            pltpu.VMEM((AXES, SIDE, SIDE, SIDE, CORES, BLOCK), jnp.int32),
            pltpu.SemaphoreType.DMA((AXES, SIDE - 1)),
            pltpu.SemaphoreType.DMA((AXES, SIDE - 1)),
            *held(sizes_in),
            *staged(sizes_in),
            *held(sizes_out),
            *staged(sizes_out),
            columns(sizes_in),
            columns(sizes_out),
            *sems(),
            *sems(),
        ],
        compiler_params=pltpu.CompilerParams(
            collective_id=0, has_side_effects=True, vmem_limit_bytes=VMEM_LIMIT
        ),
    )(
        features.T,
        w_inner,
        bias_inner.reshape(hidden, 1),
        jnp.pad(w_outer.T, ((0, padded - classes), (0, 0))),
        jnp.pad(bias_outer, (0, padded - classes)).reshape(padded, 1),
        tiles,
        tile_col,
        degrees.reshape(1, rows),
        send,
    ).T


def solution(mesh):
    return jax.shard_map(
        on_device,
        mesh=mesh,
        in_specs=(
            P(("dom", "sub"), None),
            P(),
            P(),
            P(),
            P(),
            P(("dom", "sub"), None, None, None),
            P(("dom", "sub"), None),
            P(("dom", "sub")),
            P(("dom", "sub"), None, None),
        ),
        out_specs=P(("dom", "sub"), None),
        check_vma=False,
    )
```

time: 437 us -> 160 us (0.37)
  local copies, waits for them, and re-layouts: 181 us -> 5.79 us
  Pallas kernels: 0 us -> 154 us
  waiting for transfers between devices: 152 us -> 0 us
  other arithmetic: 44.1 us -> 0 us
  matrix products: 33.7 us -> 0 us
  starting transfers between devices: 23.8 us -> 0 us
    gather x18 -> x0, local copies, waits for them, and re-layouts: 181 us -> none  [the longest x2 123 us: aggregate(): jnp.take(feature_rows, clipped, axis=0)]
    pallas_call x0 -> x1, Pallas kernels: none -> 154 us  [on_device(): pl.pallas_call(functools.partial(kernel, sizes_in, sizes_out), out_shape=...]
    all_to_all x2 -> x0, waiting for transfers between devices: 152 us -> none  [the longest x1 98.9 us: deliver_inner(): lax.all_to_all(outgoing, ('dom', 'sub'), split_axis=0, concat_axis=0, til...]
    dot_general x18 -> x0, matrix products: 33.7 us -> none  [the longest x16 31.8 us: rowblock(): jnp.einsum('tij,tjw->iw', tile_set, blocks, preferred_element_type=jnp.fl...]
    select_n x18 -> x0, other arithmetic: 26.2 us -> none  [the longest x2 15.1 us: aggregate(): jnp.where(live_slot, jnp.take(feature_rows, clipped, axis=0), jnp.zeros((...]
    all_to_all x2 -> x0, starting transfers between devices: 23.8 us -> none  [the longest x1 11.9 us: deliver_inner(): lax.all_to_all(outgoing, ('dom', 'sub'), split_axis=0, concat_axis=0, til...]
    concatenate x2 -> x0, other arithmetic: 12.2 us -> none  [aggregate(): jnp.concatenate([feature_rows.reshape(-1, block_rows, width), arrived], a...]
  transfers between devices with their start and end apart: 2 -> 0, of which waited for: 2 -> 0; matrix products, arithmetic and copies ran while one was open for 0% -> 0% of each run, Pallas kernels for 0% -> 0%
where the time goes in v2:
time: 160 us
  Pallas kernels  154 us (96%)
  local copies, waits for them, and re-layouts  5.79 us (4%)
    pallas_call x1, Pallas kernels, on_device(): pl.pallas_call(functools.partial(kernel, sizes_in, sizes_out), out_shape=...  154 us

profile of v2, /device:TPU:1, one launch (start us, length us, event | category | flops | bytes accessed | tf_op | source)
XLA Modules:
  0.0 159.6 jit_solution(13998989914070124314)
XLA Ops:
  0.0 0.7 pad_bitcast_fusion
  0.7 0.7 copy.12.refs_4_
  1.4 1.3 pad.8.refs_3_
  2.7 1.5 copy.11.refs_2_
  4.2 153.8 %shard_map.91 = f32[41,1024]{1,0:T(8,128)} custom-call(bf16[602,1024]{1,0:T(8,128)(2,1)} %bitcast.8, bf16[602,256]{1,0:T(8,128)(2,1)} %refs_1_.1, f32[256,1]{1,0:T(8,128)} %copy.11.refs_2_, bf16[48,256]{1,0:T(8,128)(2,1)} %pad.8.refs_3_, f32[48,1]{1,0:T(8,128)} %copy.12.refs_4_, bf16[8,32,128,128]{3,2,1,0:T(8,128)(2,1)} %refs_5_.1, s32[8,32]{1,0:T(8,128)} %refs_6_.1, ...), custom_call_target="tpu_custom_call" | custom-call | tf_op jit(solution)/shard_map/pallas_call | solution.py:315
  158.0 1.6 %copy.14 = f32[1024,41]{0,1:T(8,128)} copy(f32[1024,41]{0,1:T(8,128)} %bitcast.9) | data formatting | bytes 335872

commit v3 on v2

v3 whole, which is shorter than its diff:
```python
import functools

import jax
import jax.numpy as jnp
from jax import lax
from jax.experimental import pallas as pl
from jax.experimental.pallas import tpu as pltpu
from jax.sharding import PartitionSpec as P

BLOCK = 128
CHUNK = 256
SIDE = 4
CORES = 2
AXES = 3
CHIPS = SIDE * SIDE
PLANE = CHIPS * CORES
MESH = pl.DeviceIdType.MESH
VMEM_LIMIT = 60 * 1024 * 1024


def pick_rows(stacked, lists, width):
    parts = stacked.shape[0] // width
    index = jnp.concatenate([lists[0:1], lists[1:2]], axis=1)
    low = index & (CHUNK - 1)
    high = lax.shift_right_arithmetic(index, 8)
    lane = lax.broadcasted_iota(jnp.int32, (CHUNK, 2 * BLOCK), 0)
    onehot = jnp.where(lane == low, 1.0, 0.0).astype(jnp.bfloat16)
    found = jnp.dot(stacked, onehot, preferred_element_type=jnp.float32)
    total = jnp.zeros((width, 2 * BLOCK), jnp.float32)
    for part in range(parts):
        total = jnp.where(high == part, found[part * width : (part + 1) * width], total)
    return total.astype(jnp.bfloat16)


class Place:
    def __init__(self):
        dom, sub = lax.axis_index("dom"), lax.axis_index("sub")
        self.at = (dom // SIDE, dom % SIDE, sub // CORES)
        self.core = sub % CORES

    def turned(self, f):
        return [self.at[(f + k) % AXES] for k in range(AXES)]

    def device(self, f, a, b, c, core):
        x, y, z = natural(f, a, b, c)
        return (x * SIDE + y, z * CORES + core)


def natural(f, a, b, c):
    spot = [None] * AXES
    for k, value in enumerate((a, b, c)):
        spot[(f + k) % AXES] = value
    return tuple(spot)


def remote(source, there, sent, got, device):
    return pltpu.make_async_remote_copy(
        src_ref=source,
        dst_ref=there,
        send_sem=sent,
        recv_sem=got,
        device_id=device,
        device_id_type=MESH,
    )


class Exchange:
    def __init__(self, place, sizes, held, lists, staged, columns, sems):
        self.place, self.sizes, self.held, self.lists = place, sizes, held, lists
        self.staged, self.columns = staged, columns
        self.line, self.near, self.far, self.last = sems
        self.starts = [sum(sizes[:f]) for f in range(AXES)]

    def along_line(self, f, step):
        a, b, c = self.place.turned(f)
        block = self.held[f].at[b, a]
        sems = [self.line.at[k, f, step - 1] for k in range(2)]
        return remote(block, block, *sems, self.place.device(f, (a + step) % SIDE, b, c, self.place.core))

    def to_near(self, f, way, step):
        a, b, c = self.place.turned(f)
        block = self.held[f].at[b, (a + step) % SIDE]
        sems = [self.near.at[k, f, way, step] for k in range(2)]
        there = (b + 1 + 2 * way) % SIDE
        return remote(block, block, *sems, self.place.device(f, a, there, c, self.place.core))

    def to_far(self, f, step):
        a, b, c = self.place.turned(f)
        way = step % 2
        block = self.held[f].at[(b + 3 + 2 * way) % SIDE, (a + step) % SIDE]
        sems = [self.far.at[k, f, step] for k in range(2)]
        there = (b + 1 + 2 * way) % SIDE
        return remote(block, block, *sems, self.place.device(f, a, there, c, self.place.core))

    def to_last(self, f, spot, core, sender, device):
        a, b, c = self.place.turned(f)
        x, y, z = natural(f, pl.ds(0, SIDE), (b + spot // SIDE) % SIDE, c)
        there = self.columns.at[x, y, z, self.place.core, pl.ds(self.starts[f], self.sizes[f]), :]
        return remote(
            self.staged[f].at[spot * CORES + core],
            there,
            self.last.at[0, f, spot * CORES + core],
            self.last.at[1, f, spot * CORES + sender],
            self.place.device(f, a, b, (c + spot % SIDE) % SIDE, device),
        )

    def leaves(self, spot, core):
        return jnp.logical_or(spot % SIDE != 0, self.place.core != core)

    def start(self):
        for step in range(1, SIDE):
            for f in range(AXES):
                self.along_line(f, step).start()
        for way in range(2):
            for f in range(AXES):
                self.to_near(f, way, 0).start()

    def run(self):
        for step in range(1, SIDE):
            for f in range(AXES):
                self.along_line(f, SIDE - step).wait()
            for way in range(2):
                for f in range(AXES):
                    self.to_near(f, way, step).start()
        self.pick(0, SIDE)
        for step in range(SIDE):
            for way in range(2):
                for f in range(AXES):
                    self.to_near(f, way, step).wait()
            for f in range(AXES):
                self.to_far(f, step).start()
        self.pick(SIDE, 2 * SIDE)
        for step in range(SIDE):
            for f in range(AXES):
                self.to_far(f, step).wait()
        self.pick(3 * SIDE, SIDE)
        self.finish()

    def pick(self, first, count):
        p = self.place

        @pl.loop(first, first + count)
        def _(turn):
            row = turn // SIDE
            row = row + jnp.where(row == 2, 1, 0) - jnp.where(row == 3, 1, 0)
            ahead = (turn + 1) % SIDE
            spot = row * SIDE + ahead
            for f in range(AXES):
                a, b, c = p.turned(f)
                b, c = (b + row) % SIDE, (c + ahead) % SIDE
                for k in range(SIDE):
                    picked = pick_rows(self.held[f][b, k], self.lists[f, b, k, c], self.sizes[f])
                    self.staged[f][spot * CORES, k] = picked[:, :BLOCK]
                    self.staged[f][spot * CORES + 1, k] = picked[:, BLOCK:]
                for core in range(CORES):

                    @pl.when(self.leaves(spot, core))
                    def _():
                        self.to_last(f, spot, core, p.core, core).start()

    def finish(self):
        p = self.place
        for f in range(AXES):
            a, b, c = p.turned(f)
            rows = pl.ds(self.starts[f], self.sizes[f])
            for row in range(SIDE):
                for k in range(SIDE):
                    x, y, z = natural(f, k, (b + row) % SIDE, c)
                    self.columns[x, y, z, p.core, rows, :] = self.staged[f][row * PLANE // SIDE + p.core, k]

        @pl.loop(0, CHIPS)
        def _(spot):
            for f in range(AXES):
                for core in range(CORES):

                    @pl.when(self.leaves(spot, core))
                    def _():
                        self.to_last(f, spot, core, p.core, core).wait_send()
                        self.to_last(f, spot, core, core, 1 - p.core).wait_recv()


def summed(tile_col, tiles, columns, row):
    total = None

    def column(t):
        c = (tile_col[row, t] + SIDE * PLANE) % (SIDE * PLANE + 8)
        return columns[c // PLANE, (c // 8) % SIDE, (c // CORES) % SIDE, c % CORES]

    for pair in range(tiles.shape[1] // 2):
        rows = jnp.concatenate([column(2 * pair), column(2 * pair + 1)], axis=1)
        edges = jnp.concatenate([tiles[row, 2 * pair], tiles[row, 2 * pair + 1]], axis=1)
        product = lax.dot_general(
            rows, edges, (((1,), (1,)), ((), ())), preferred_element_type=jnp.float32
        )
        total = product if total is None else total + product
    return total


def kernel(sizes_in, sizes_out, *refs):
    (features, w_inner, bias_inner, w_outer, bias_outer, tiles_far, tile_col, degrees, send) = refs[:9]
    logits = refs[9]
    scratch = list(refs[10:])
    tiles, tiles_sem, lists, list_sems = scratch[:4]
    held_in, staged_in = scratch[4:7], scratch[7:10]
    held_out, staged_out = scratch[10:13], scratch[13:16]
    columns_in, columns_out = scratch[16:18]
    sems_in, sems_out = scratch[18:22], scratch[22:26]

    place = Place()
    load = pltpu.make_async_copy(tiles_far, tiles, tiles_sem)
    load.start()

    barrier = pltpu.get_barrier_semaphore()

    def greet(device):
        pl.semaphore_signal(barrier, inc=1, device_id=device, device_id_type=MESH)

    for f in range(AXES):
        a, b, c = place.turned(f)
        for spot in range(1, CHIPS):
            greet(place.device(f, (a + spot // SIDE) % SIDE, (b + spot % SIDE) % SIDE, c, place.core))
        for step in range(1, SIDE):
            greet(place.device(f, a, b, (c + step) % SIDE, 1 - place.core))
    greet(place.device(0, *place.at, 1 - place.core))

    def lists_to(f, spot):
        a, b, c = place.turned(f)
        there = ((a + spot // SIDE) % SIDE, (b + spot % SIDE) % SIDE)
        return remote(
            send.at[natural(f, *there, slice(None))],
            lists.at[f, b, a],
            list_sems.at[0, f, spot],
            list_sems.at[1, f, spot],
            place.device(f, *there, c, place.core),
        )

    inner = Exchange(place, sizes_in, held_in, lists, staged_in, columns_in, sems_in)
    outer = Exchange(place, sizes_out, held_out, lists, staged_out, columns_out, sems_out)

    def keep(exchange, part, piece):
        for f in range(AXES):
            size = exchange.sizes[f]
            rows = piece[exchange.starts[f] : exchange.starts[f] + size]
            a, b, c = place.turned(f)
            exchange.held[f][b, a, pl.ds(part * size, size), :] = rows
        exchange.columns[SIDE, 0, part, 0] = piece[:, :BLOCK]
        exchange.columns[SIDE, 0, part, 1] = piece[:, BLOCK:]

    def scale(part):
        return lax.rsqrt(degrees[:, pl.ds(part * CHUNK, CHUNK)].astype(jnp.float32))

    for part in range(SIDE):
        product = lax.dot_general(
            w_inner[...],
            features[:, part * CHUNK : (part + 1) * CHUNK],
            (((0,), (0,)), ((), ())),
            preferred_element_type=jnp.float32,
        )
        keep(inner, part, (product * scale(part)).astype(jnp.bfloat16))

    for f in range(AXES):
        a, b, c = place.turned(f)
        x, y, z = natural(f, a, b, slice(None))
        lists[f, b, a] = send[x, y, z]

    pl.semaphore_wait(barrier, AXES * (CHIPS - 1 + SIDE - 1) + 1)
    for f in range(AXES):
        for spot in range(1, CHIPS):
            lists_to(f, spot).start()
    inner.start()
    for f in range(AXES):
        for spot in range(1, CHIPS):
            lists_to(f, spot).wait()
    inner.run()

    load.wait()

    @pl.loop(0, SIDE)
    def _(part):
        inv_sqrt = scale(part)
        aggregated = jnp.concatenate(
            [summed(tile_col, tiles, columns_in, 2 * part + half) for half in range(2)], axis=1
        )
        hidden = inv_sqrt * jnp.maximum(inv_sqrt * aggregated + bias_inner[...], 0.0)
        result = jnp.dot(w_outer[...], hidden.astype(jnp.bfloat16), preferred_element_type=jnp.float32)
        keep(outer, part, result.astype(jnp.bfloat16))

    outer.start()
    outer.run()

    @pl.loop(0, SIDE)
    def _(part):
        aggregated = jnp.concatenate(
            [summed(tile_col, tiles, columns_out, 2 * part + half) for half in range(2)], axis=1
        )
        result = scale(part) * aggregated + bias_outer[...]
        logits[:, pl.ds(part * CHUNK, CHUNK)] = result[: logits.shape[0]]


def on_device(features, w_inner, bias_inner, w_outer, bias_outer, tiles, tile_col, degrees, send_rows):
    rows, _ = features.shape
    hidden = w_inner.shape[1]
    classes = w_outer.shape[1]
    padded = 16 * AXES
    sizes_in, sizes_out = (96, 80, 80), (16, 16, 16)
    send = send_rows.reshape(SIDE, SIDE, SIDE, CORES, BLOCK)
    vmem = pl.BlockSpec(memory_space=pltpu.VMEM)
    bf16 = jnp.bfloat16

    def held(sizes):
        return [pltpu.VMEM((SIDE, SIDE, SIDE * size, CHUNK), bf16) for size in sizes]

    def staged(sizes):
        return [pltpu.VMEM((PLANE, SIDE, size, BLOCK), bf16) for size in sizes]

    def columns(sizes):
        return pltpu.VMEM((SIDE + 1, SIDE, SIDE, CORES, sum(sizes), BLOCK), bf16)

    def sems():
        shapes = [(SIDE - 1,), (2, SIDE), (SIDE,), (PLANE,)]
        return [pltpu.SemaphoreType.DMA((2, AXES, *shape)) for shape in shapes]

    return pl.pallas_call(
        functools.partial(kernel, sizes_in, sizes_out),
        out_shape=jax.ShapeDtypeStruct((classes, rows), jnp.float32),
        in_specs=[
            vmem,
            vmem,
            vmem,
            vmem,
            vmem,
            pl.BlockSpec(memory_space=pl.ANY),
            pl.BlockSpec(memory_space=pltpu.SMEM),
            vmem,
            vmem,
        ],
        out_specs=vmem,
        scratch_shapes=[
            pltpu.VMEM(tiles.shape, bf16),
            pltpu.SemaphoreType.DMA,
            pltpu.VMEM((AXES, SIDE, SIDE, SIDE, CORES, BLOCK), jnp.int32),
            pltpu.SemaphoreType.DMA((2, AXES, CHIPS)),
            *held(sizes_in),
            *staged(sizes_in),
            *held(sizes_out),
            *staged(sizes_out),
            columns(sizes_in),
            columns(sizes_out),
            *sems(),
            *sems(),
        ],
        compiler_params=pltpu.CompilerParams(
            collective_id=0, has_side_effects=True, vmem_limit_bytes=VMEM_LIMIT
        ),
    )(
        features.T,
        w_inner,
        bias_inner.reshape(hidden, 1),
        jnp.pad(w_outer.T, ((0, padded - classes), (0, 0))),
        jnp.pad(bias_outer, (0, padded - classes)).reshape(padded, 1),
        tiles,
        tile_col,
        degrees.reshape(1, rows),
        send,
    ).T


def solution(mesh):
    return jax.shard_map(
        on_device,
        mesh=mesh,
        in_specs=(
            P(("dom", "sub"), None),
            P(),
            P(),
            P(),
            P(),
            P(("dom", "sub"), None, None, None),
            P(("dom", "sub"), None),
            P(("dom", "sub")),
            P(("dom", "sub"), None, None),
        ),
        out_specs=P(("dom", "sub"), None),
        check_vma=False,
    )
```

time: 160 us -> 121 us (0.76)
  Pallas kernels: 154 us -> 115 us
    pallas_call x1, Pallas kernels: 154 us -> 115 us  [on_device(): pl.pallas_call(functools.partial(kernel, sizes_in, sizes_out), out_shape=...]
where the time goes in v3:
time: 121 us
  Pallas kernels  115 us (95%)
  local copies, waits for them, and re-layouts  5.79 us (5%)
    pallas_call x1, Pallas kernels, on_device(): pl.pallas_call(functools.partial(kernel, sizes_in, sizes_out), out_shape=...  115 us

profile of v3, /device:TPU:1, one launch (start us, length us, event | category | flops | bytes accessed | tf_op | source)
XLA Modules:
  0.0 120.9 jit_solution(10028387720682074436)
XLA Ops:
  0.0 0.7 pad_bitcast_fusion
  0.7 0.7 copy.12.refs_4_
  1.4 1.3 %pad.8.refs_3_ = bf16[48,256]{1,0:T(8,128)(2,1)} pad(bf16[41,256]{1,0:T(8,128)(2,1)} %bitcast.11, bf16[]{:T(256)} %constant.3.clone.1), padding=0_7x0_0 | pad | bytes 45570 | tf_op jit(solution)/shard_map/jit(_pad)/pad | solution.py:359
  2.7 1.5 %copy.11.refs_2_ = f32[256,1]{1,0:T(8,128)} copy(f32[256,1]{0,1:T(1,128)} %bitcast.13) | data formatting | bytes 2048 | tf_op jit(solution)/shard_map/reshape | solution.py:358
  4.2 115.1 %shard_map.91 = f32[41,1024]{1,0:T(8,128)} custom-call(bf16[602,1024]{1,0:T(8,128)(2,1)} %bitcast.8, bf16[602,256]{1,0:T(8,128)(2,1)} %refs_1_.1, f32[256,1]{1,0:T(8,128)} %copy.11.refs_2_, bf16[48,256]{1,0:T(8,128)(2,1)} %pad.8.refs_3_, f32[48,1]{1,0:T(8,128)} %copy.12.refs_4_, bf16[8,32,128,128]{3,2,1,0:T(8,128)(2,1)} %refs_5_.1, s32[8,32]{1,0:T(8,128)} %refs_6_.1, ...), custom_call_target="tpu_custom_call" | custom-call | tf_op jit(solution)/shard_map/pallas_call | solution.py:323
  119.2 1.6 %copy.14 = f32[1024,41]{0,1:T(8,128)} copy(f32[1024,41]{0,1:T(8,128)} %bitcast.9) | data formatting | bytes 335872

commit v4 on v3

v4 whole, which is shorter than its diff:
```python
import functools

import jax
import jax.numpy as jnp
from jax import lax
from jax.experimental import pallas as pl
from jax.experimental.pallas import tpu as pltpu
from jax.sharding import PartitionSpec as P

BLOCK = 128
CHUNK = 256
SIDE = 4
CORES = 2
AXES = 3
CHIPS = SIDE * SIDE
PLANE = CHIPS * CORES
MESH = pl.DeviceIdType.MESH
VMEM_LIMIT = 60 * 1024 * 1024


def pick_rows(stacked, lists, width):
    parts, chunk = stacked.shape[0] // width, stacked.shape[1]
    index = jnp.concatenate([lists[0:1], lists[1:2]], axis=1)
    low = index & (chunk - 1)
    high = lax.shift_right_arithmetic(index, chunk.bit_length() - 1)
    lane = lax.broadcasted_iota(jnp.int32, (chunk, 2 * BLOCK), 0)
    onehot = jnp.where(lane == low, 1.0, 0.0).astype(jnp.bfloat16)
    found = jnp.dot(stacked, onehot, preferred_element_type=jnp.float32)
    total = jnp.zeros((width, 2 * BLOCK), jnp.float32)
    for part in range(parts):
        total = jnp.where(high == part, found[part * width : (part + 1) * width], total)
    return total.astype(jnp.bfloat16)


class Place:
    def __init__(self):
        dom, sub = lax.axis_index("dom"), lax.axis_index("sub")
        self.at = (dom // SIDE, dom % SIDE, sub // CORES)
        self.core = sub % CORES

    def turned(self, f):
        return [self.at[(f + k) % AXES] for k in range(AXES)]

    def device(self, f, a, b, c, core):
        x, y, z = natural(f, a, b, c)
        return (x * SIDE + y, z * CORES + core)


def natural(f, a, b, c):
    spot = [None] * AXES
    for k, value in enumerate((a, b, c)):
        spot[(f + k) % AXES] = value
    return tuple(spot)


def remote(source, there, sent, got, device):
    return pltpu.make_async_remote_copy(
        src_ref=source,
        dst_ref=there,
        send_sem=sent,
        recv_sem=got,
        device_id=device,
        device_id_type=MESH,
    )


class Exchange:
    def __init__(self, place, sizes, held, lists, staged, columns, sems):
        self.place, self.sizes, self.held, self.lists = place, sizes, held, lists
        self.staged, self.columns = staged, columns
        self.held_sent, self.last_sent, self.line, self.near, self.far, self.last = sems
        self.starts = [sum(sizes[:f]) for f in range(AXES)]

    def along_line(self, f, step):
        a, b, c = self.place.turned(f)
        block = self.held[f].at[b * SIDE + a]
        sems = self.held_sent.at[f], self.line.at[f, step - 1]
        return remote(block, block, *sems, self.place.device(f, (a + step) % SIDE, b, c, self.place.core))

    def to_near(self, f, way, step):
        a, b, c = self.place.turned(f)
        block = self.held[f].at[b * SIDE + (a + step) % SIDE]
        sems = self.held_sent.at[f], self.near.at[f, way, step]
        there = (b + 1 + 2 * way) % SIDE
        return remote(block, block, *sems, self.place.device(f, a, there, c, self.place.core))

    def to_far(self, f, step):
        a, b, c = self.place.turned(f)
        way = step % 2
        block = self.held[f].at[(b + 3 + 2 * way) % SIDE * SIDE + (a + step) % SIDE]
        sems = self.held_sent.at[f], self.far.at[f, step]
        there = (b + 1 + 2 * way) % SIDE
        return remote(block, block, *sems, self.place.device(f, a, there, c, self.place.core))

    def to_last(self, f, spot, core):
        a, b, c = self.place.turned(f)
        x, y, z = natural(f, pl.ds(0, SIDE), (b + spot // SIDE) % SIDE, c)
        there = self.columns.at[x, y, z, self.place.core, pl.ds(self.starts[f], self.sizes[f]), :]
        return remote(
            self.staged[f].at[spot * CORES + core],
            there,
            self.last_sent.at[f],
            self.last.at[f],
            self.place.device(f, a, b, (c + spot % SIDE) % SIDE, core),
        )

    def leaves(self, spot, core):
        return jnp.logical_or(spot % SIDE != 0, self.place.core != core)

    def start(self):
        for step in range(1, SIDE):
            for f in range(AXES):
                self.along_line(f, step).start()
        for way in range(2):
            for f in range(AXES):
                self.to_near(f, way, 0).start()

    def run(self, ready=lambda: None):
        for step in range(1, SIDE):
            for f in range(AXES):
                self.along_line(f, SIDE - step).wait_recv()
            for way in range(2):
                for f in range(AXES):
                    self.to_near(f, way, step).start()
        ready()
        self.pick(0, SIDE)
        for step in range(SIDE):
            for way in range(2):
                for f in range(AXES):
                    self.to_near(f, way, step).wait_recv()
            for f in range(AXES):
                self.to_far(f, step).start()
        self.pick(SIDE, 2 * SIDE)
        for step in range(SIDE):
            for f in range(AXES):
                self.to_far(f, step).wait_recv()
        self.pick(3 * SIDE, SIDE)
        self.finish()

    def pick(self, first, count):
        p = self.place

        @pl.loop(first, first + count)
        def _(turn):
            row = turn // SIDE
            row = row + jnp.where(row == 2, 1, 0) - jnp.where(row == 3, 1, 0)
            ahead = (turn + 1) % SIDE
            spot = row * SIDE + ahead
            for f in range(AXES):
                a, b, c = p.turned(f)
                b, c = (b + row) % SIDE, (c + ahead) % SIDE
                for k in range(SIDE):
                    picked = pick_rows(self.held[f][b * SIDE + k], self.lists[f, b, k, c], self.sizes[f])
                    self.staged[f][spot * CORES, k] = picked[:, :BLOCK]
                    self.staged[f][spot * CORES + 1, k] = picked[:, BLOCK:]
                for core in range(CORES):

                    @pl.when(self.leaves(spot, core))
                    def _():
                        self.to_last(f, spot, core).start()

    def finish(self):
        p = self.place
        for f in range(AXES):
            a, b, c = p.turned(f)
            rows = pl.ds(self.starts[f], self.sizes[f])
            for row in range(SIDE):
                for k in range(SIDE):
                    x, y, z = natural(f, k, (b + row) % SIDE, c)
                    self.columns[x, y, z, p.core, rows, :] = self.staged[f][row * PLANE // SIDE + p.core, k]

        for f in range(AXES):
            a, b, c = p.turned(f)
            device = p.device(f, a, b, c, 1 - p.core)
            held = self.held[f].at[pl.ds(0, CHIPS - 1)]
            picked = self.staged[f].at[pl.ds(0, PLANE - SIDE)]
            remote(held, held, self.held_sent.at[f], self.last.at[f], device).wait_send()
            last = remote(picked, picked, self.last_sent.at[f], self.last.at[f], device)
            last.wait_send()
            last.wait_recv()


def summed(tile_col, tiles, columns, row, swap):
    total = None

    def column(t):
        c = (tile_col[row, t] + SIDE * PLANE) % (SIDE * PLANE + 8)
        return columns[c // PLANE, (c // 8) % SIDE, (c // CORES) % SIDE, c % CORES]

    for pair in range(tiles.shape[1] // 2):
        rows = jnp.concatenate([column(2 * pair), column(2 * pair + 1)], axis=1)
        edges = jnp.concatenate([tiles[row, 2 * pair], tiles[row, 2 * pair + 1]], axis=1)
        operands = (edges, rows) if swap else (rows, edges)
        product = lax.dot_general(
            *operands, (((1,), (1,)), ((), ())), preferred_element_type=jnp.float32
        )
        total = product if total is None else total + product
    return total


def down(row):
    return jnp.transpose(jnp.broadcast_to(row, (BLOCK, row.shape[1])))


def kernel(sizes_in, sizes_out, *refs):
    (features_far, w_far, bias_inner, w_outer, bias_outer, tiles_far, tile_col, degrees, send) = refs[:9]
    logits = refs[9]
    scratch = list(refs[10:])
    tiles, tiles_sem, lists, halfway = scratch[:4]
    held_in, staged_in = scratch[4:7], scratch[7:10]
    held_out, staged_out = scratch[10:13], scratch[13:16]
    columns_in, columns_out = scratch[16:18]
    features, w_inner, few_sems, list_sent, list_got, held_sent, last_sent = scratch[18:25]
    sems_in = held_sent, last_sent, *scratch[25:29]
    sems_out = held_sent, last_sent, *scratch[29:33]

    place = Place()
    load_w = pltpu.make_async_copy(w_far, w_inner, few_sems.at[0])
    load_features = pltpu.make_async_copy(features_far, features, few_sems.at[1])
    load = pltpu.make_async_copy(tiles_far, tiles, tiles_sem)
    load_w.start()
    load_features.start()
    load.start()

    barrier = pltpu.get_barrier_semaphore()

    def greet(device):
        pl.semaphore_signal(barrier, inc=1, device_id=device, device_id_type=MESH)

    for f in range(AXES):
        a, b, c = place.turned(f)
        for step in range(1, SIDE):
            for core in range(CORES):
                greet(place.device(f, (a + step) % SIDE, b, c, core))
    greet(place.device(0, *place.at, 1 - place.core))

    def lists_along(f, step):
        a, b, c = place.turned(f)
        there = (a + step) % SIDE
        cut = [slice(None)] * AXES
        cut[f] = there
        return remote(
            send.at[tuple(cut)],
            halfway.at[f, a],
            list_sent.at[0, f],
            list_got.at[0, f],
            place.device(f, there, b, c, place.core),
        )

    def cut_lists(f, b):
        return (f, slice(None), slice(None), b) if f == 1 else (f, slice(None), b)

    def lists_across(f, step):
        a, b, c = place.turned(f)
        there = (b + step) % SIDE
        return remote(
            halfway.at[cut_lists(f, there)],
            lists.at[f, b],
            list_sent.at[1, f],
            list_got.at[1, f],
            place.device(f, a, there, c, place.core),
        )

    def lists_done(f, stage, buffer):
        three = buffer.at[f, pl.ds(0, SIDE - 1)]
        device = place.device(0, *place.at, 1 - place.core)
        return remote(three, three, list_sent.at[stage, f], list_got.at[stage, f], device)

    for f in range(AXES):
        a, b, c = place.turned(f)
        cut = [slice(None)] * AXES
        cut[f] = a
        halfway[f, a] = send[tuple(cut)]

    pl.semaphore_wait(barrier, AXES * (SIDE - 1) * CORES + 1)
    for f in range(AXES):
        for step in range(1, SIDE):
            lists_along(f, step).start()

    def lists_middle():
        for f in range(AXES):
            lists_done(f, 0, halfway).wait_recv()
            for step in range(1, SIDE):
                lists_across(f, step).start()
            a, b, c = place.turned(f)
            lists[f, b] = halfway[cut_lists(f, b)]

    def lists_ready():
        for f in range(AXES):
            lists_done(f, 0, halfway).wait_send()
            lists_done(f, 1, lists).wait()

    inner = Exchange(place, sizes_in, held_in, lists, staged_in, columns_in, sems_in)
    outer = Exchange(place, sizes_out, held_out, lists, staged_out, columns_out, sems_out)

    def keep(exchange, part, piece):
        chunk = exchange.held[0].shape[2]
        for f in range(AXES):
            size = exchange.sizes[f]
            rows = piece[exchange.starts[f] : exchange.starts[f] + size]
            a, b, c = place.turned(f)
            for k in range(CHUNK // chunk):
                at = pl.ds((part * (CHUNK // chunk) + k) * size, size)
                exchange.held[f][b * SIDE + a, at, :] = rows[:, k * chunk : (k + 1) * chunk]
        exchange.columns[SIDE, 0, part, 0] = piece[:, :BLOCK]
        exchange.columns[SIDE, 0, part, 1] = piece[:, BLOCK:]

    def scale(start, size):
        return lax.rsqrt(degrees[:, pl.ds(start, size)].astype(jnp.float32))

    load_w.wait()
    w_turned = jnp.transpose(w_inner[...])
    load_features.wait()
    for part in range(SIDE):
        product = jnp.dot(
            w_turned,
            features[:, part * CHUNK : (part + 1) * CHUNK],
            preferred_element_type=jnp.float32,
        )
        keep(inner, part, (product * scale(part * CHUNK, CHUNK)).astype(jnp.bfloat16))

    inner.start()
    lists_middle()
    inner.run(lists_ready)

    load.wait()
    bias_down = down(bias_inner[...])

    @pl.loop(0, SIDE)
    def _(part):
        hidden = []
        for half in range(2):
            inv_sqrt = scale((2 * part + half) * BLOCK, BLOCK)
            aggregated = summed(tile_col, tiles, columns_in, 2 * part + half, False)
            hidden.append(inv_sqrt * jnp.maximum(inv_sqrt * aggregated + bias_down, 0.0))
        hidden = jnp.concatenate(hidden, axis=1).astype(jnp.bfloat16)
        result = jnp.dot(w_outer[...], hidden, preferred_element_type=jnp.float32)
        spare = jnp.zeros((sum(sizes_out) - result.shape[0], CHUNK), jnp.float32)
        keep(outer, part, jnp.concatenate([result, spare], axis=0).astype(jnp.bfloat16))

    outer.start()
    outer.run()
    last_down = down(bias_outer[...])

    @pl.loop(0, SIDE)
    def _(part):
        for half in range(2):
            start = (2 * part + half) * BLOCK
            aggregated = jnp.transpose(summed(tile_col, tiles, columns_out, 2 * part + half, True))
            logits[:, pl.ds(start, BLOCK)] = scale(start, BLOCK) * aggregated[: logits.shape[0]] + last_down


def on_device(features, w_inner, bias_inner, w_outer, bias_outer, tiles, tile_col, degrees, send_rows):
    rows, _ = features.shape
    hidden = w_inner.shape[1]
    classes = w_outer.shape[1]
    sizes_in, sizes_out = (96, 80, 80), (16, 16, 16)
    send = send_rows.reshape(SIDE, SIDE, SIDE, CORES, BLOCK)
    vmem = pl.BlockSpec(memory_space=pltpu.VMEM)
    bf16 = jnp.bfloat16

    def held(sizes, chunk):
        return [pltpu.VMEM((CHIPS, rows // chunk * size, chunk), bf16) for size in sizes]

    def staged(sizes):
        return [pltpu.VMEM((PLANE, SIDE, size, BLOCK), bf16) for size in sizes]

    def columns(sizes):
        return pltpu.VMEM((SIDE + 1, SIDE, SIDE, CORES, sum(sizes), BLOCK), bf16)

    def sems():
        shapes = [(SIDE - 1,), (2, SIDE), (SIDE,), ()]
        return [pltpu.SemaphoreType.DMA((AXES, *shape)) for shape in shapes]

    return pl.pallas_call(
        functools.partial(kernel, sizes_in, sizes_out),
        out_shape=jax.ShapeDtypeStruct((classes, rows), jnp.float32),
        in_specs=[
            pl.BlockSpec(memory_space=pl.ANY),
            pl.BlockSpec(memory_space=pl.ANY),
            vmem,
            vmem,
            vmem,
            pl.BlockSpec(memory_space=pl.ANY),
            pl.BlockSpec(memory_space=pltpu.SMEM),
            vmem,
            vmem,
        ],
        out_specs=vmem,
        scratch_shapes=[
            pltpu.VMEM(tiles.shape, bf16),
            pltpu.SemaphoreType.DMA,
            pltpu.VMEM((AXES, SIDE, SIDE, SIDE, CORES, BLOCK), jnp.int32),
            pltpu.VMEM((AXES, SIDE, SIDE, SIDE, CORES, BLOCK), jnp.int32),
            *held(sizes_in, CHUNK),
            *staged(sizes_in),
            *held(sizes_out, BLOCK),
            *staged(sizes_out),
            columns(sizes_in),
            columns(sizes_out),
            pltpu.VMEM((features.shape[1], rows), bf16),
            pltpu.VMEM(w_inner.shape, bf16),
            pltpu.SemaphoreType.DMA((2,)),
            pltpu.SemaphoreType.DMA((2, AXES)),
            pltpu.SemaphoreType.DMA((2, AXES)),
            pltpu.SemaphoreType.DMA((AXES,)),
            pltpu.SemaphoreType.DMA((AXES,)),
            *sems(),
            *sems(),
        ],
        compiler_params=pltpu.CompilerParams(
            collective_id=0, has_side_effects=True, vmem_limit_bytes=VMEM_LIMIT
        ),
    )(
        features.T,
        w_inner,
        bias_inner.reshape(1, hidden),
        w_outer.T,
        bias_outer.reshape(1, classes),
        tiles,
        tile_col,
        degrees.reshape(1, rows),
        send,
    ).T


def solution(mesh):
    return jax.shard_map(
        on_device,
        mesh=mesh,
        in_specs=(
            P(("dom", "sub"), None),
            P(),
            P(),
            P(),
            P(),
            P(("dom", "sub"), None, None, None),
            P(("dom", "sub"), None),
            P(("dom", "sub")),
            P(("dom", "sub"), None, None),
        ),
        out_specs=P(("dom", "sub"), None),
        check_vma=False,
    )
```

time: 121 us -> 110 us (0.909)
  Pallas kernels: 115 us -> 108 us
  local copies, waits for them, and re-layouts: 5.79 us -> 1.62 us
    pallas_call x1, Pallas kernels: 115 us -> 108 us  [on_device(): pl.pallas_call(functools.partial(kernel, sizes_in, sizes_out), out_shape=...]
    reshape x3 -> x0, local copies, waits for them, and re-layouts: 2.83 us -> none  [the longest x1 1.47 us: on_device(): bias_inner.reshape(hidden, 1)]
    pad x1 -> x0, local copies, waits for them, and re-layouts: 1.34 us -> none  [on_device(): jnp.pad(w_outer.T, ((0, padded - classes), (0, 0)))]
where the time goes in v4:
time: 110 us
  Pallas kernels  108 us (98%)
  local copies, waits for them, and re-layouts  1.62 us (1%)
    pallas_call x1, Pallas kernels, on_device(): pl.pallas_call(functools.partial(kernel, sizes_in, sizes_out), out_shape=...  108 us

profile of v4, /device:TPU:1, one launch (start us, length us, event | category | flops | bytes accessed | tf_op | source)
XLA Modules:
  0.0 109.9 jit_solution(8922843058092810065)
XLA Ops:
  0.0 108.3 %shard_map.91 = f32[41,1024]{1,0:T(8,128)} custom-call(bf16[602,1024]{1,0:T(8,128)(2,1)} %bitcast.7, bf16[602,256]{1,0:T(8,128)(2,1)} %refs_1_.1, f32[1,256]{1,0:T(1,128)} %bitcast.12, bf16[41,256]{1,0:T(8,128)(2,1)} %bitcast.10, f32[1,41]{1,0:T(1,128)} %bitcast.13, bf16[8,32,128,128]{3,2,1,0:T(8,128)(2,1)} %refs_5_.1, s32[8,32]{1,0:T(8,128)} %refs_6_.1, ...), custom_call_target="tpu_custom_call" | custom-call | tf_op jit(solution)/shard_map/pallas_call | solution.py:375
  108.3 1.6 %copy.11 = f32[1024,41]{0,1:T(8,128)} copy(f32[1024,41]{0,1:T(8,128)} %bitcast.8) | data formatting | bytes 335872

commit v5 on v4

--- a/solution.py
+++ b/solution.py
@@ -15,16 +15,20 @@
 CHIPS = SIDE * SIDE
 PLANE = CHIPS * CORES
 MESH = pl.DeviceIdType.MESH
-VMEM_LIMIT = 60 * 1024 * 1024
-
-
-def pick_rows(stacked, lists, width):
+VMEM_LIMIT = 63 * 1024 * 1024
+
+
+def pick_rows(stacked, lists, width, kept):
     parts, chunk = stacked.shape[0] // width, stacked.shape[1]
     index = jnp.concatenate([lists[0:1], lists[1:2]], axis=1)
-    low = index & (chunk - 1)
     high = lax.shift_right_arithmetic(index, chunk.bit_length() - 1)
-    lane = lax.broadcasted_iota(jnp.int32, (chunk, 2 * BLOCK), 0)
-    onehot = jnp.where(lane == low, 1.0, 0.0).astype(jnp.bfloat16)
+    if chunk == BLOCK:
+        onehot = kept[...]
+    else:
+        low = index & (chunk - 1)
+        lane = lax.broadcasted_iota(jnp.int32, (chunk, 2 * BLOCK), 0)
+        onehot = jnp.where(lane == low, 1.0, 0.0).astype(jnp.bfloat16)
+        kept[...] = onehot[:BLOCK] + onehot[BLOCK:]
     found = jnp.dot(stacked, onehot, preferred_element_type=jnp.float32)
     total = jnp.zeros((width, 2 * BLOCK), jnp.float32)
     for part in range(parts):
@@ -32,11 +36,19 @@
     return total.astype(jnp.bfloat16)
 
 
+def mod(value, by=SIDE):
+    return lax.rem(value, jnp.int32(by))
+
+
+def div(value, by=SIDE):
+    return lax.div(value, jnp.int32(by))
+
+
 class Place:
     def __init__(self):
         dom, sub = lax.axis_index("dom"), lax.axis_index("sub")
-        self.at = (dom // SIDE, dom % SIDE, sub // CORES)
-        self.core = sub % CORES
+        self.at = (div(dom), mod(dom), div(sub, CORES))
+        self.core = mod(sub, CORES)
 
     def turned(self, f):
         return [self.at[(f + k) % AXES] for k in range(AXES)]
@@ -65,7 +77,8 @@
 
 
 class Exchange:
-    def __init__(self, place, sizes, held, lists, staged, columns, sems):
+    def __init__(self, place, sizes, held, lists, kept, staged, columns, sems):
+        self.kept = kept
         self.place, self.sizes, self.held, self.lists = place, sizes, held, lists
         self.staged, self.columns = staged, columns
         self.held_sent, self.last_sent, self.line, self.near, self.far, self.last = sems
@@ -75,37 +88,37 @@
         a, b, c = self.place.turned(f)
         block = self.held[f].at[b * SIDE + a]
         sems = self.held_sent.at[f], self.line.at[f, step - 1]
-        return remote(block, block, *sems, self.place.device(f, (a + step) % SIDE, b, c, self.place.core))
+        return remote(block, block, *sems, self.place.device(f, mod(a + step), b, c, self.place.core))
 
     def to_near(self, f, way, step):
         a, b, c = self.place.turned(f)
-        block = self.held[f].at[b * SIDE + (a + step) % SIDE]
+        block = self.held[f].at[b * SIDE + mod(a + step)]
         sems = self.held_sent.at[f], self.near.at[f, way, step]
-        there = (b + 1 + 2 * way) % SIDE
+        there = mod(b + 1 + 2 * way)
         return remote(block, block, *sems, self.place.device(f, a, there, c, self.place.core))
 
     def to_far(self, f, step):
         a, b, c = self.place.turned(f)
         way = step % 2
-        block = self.held[f].at[(b + 3 + 2 * way) % SIDE * SIDE + (a + step) % SIDE]
+        block = self.held[f].at[mod(b + 3 + 2 * way) * SIDE + mod(a + step)]
         sems = self.held_sent.at[f], self.far.at[f, step]
-        there = (b + 1 + 2 * way) % SIDE
+        there = mod(b + 1 + 2 * way)
         return remote(block, block, *sems, self.place.device(f, a, there, c, self.place.core))
 
-    def to_last(self, f, spot, core):
+    def to_last(self, f, row, ahead, core):
         a, b, c = self.place.turned(f)
-        x, y, z = natural(f, pl.ds(0, SIDE), (b + spot // SIDE) % SIDE, c)
+        x, y, z = natural(f, pl.ds(0, SIDE), mod(b + row), c)
         there = self.columns.at[x, y, z, self.place.core, pl.ds(self.starts[f], self.sizes[f]), :]
         return remote(
-            self.staged[f].at[spot * CORES + core],
+            self.staged[f].at[(row * SIDE + ahead) * CORES + core],
             there,
             self.last_sent.at[f],
             self.last.at[f],
-            self.place.device(f, a, b, (c + spot % SIDE) % SIDE, core),
+            self.place.device(f, a, b, mod(c + ahead), core),
         )
 
-    def leaves(self, spot, core):
-        return jnp.logical_or(spot % SIDE != 0, self.place.core != core)
+    def leaves(self, ahead, core):
+        return jnp.logical_or(ahead != 0, self.place.core != core)
 
     def start(self):
         for step in range(1, SIDE):
@@ -142,22 +155,28 @@
 
         @pl.loop(first, first + count)
         def _(turn):
-            row = turn // SIDE
+            row = div(turn)
             row = row + jnp.where(row == 2, 1, 0) - jnp.where(row == 3, 1, 0)
-            ahead = (turn + 1) % SIDE
+            ahead = mod(turn + 1)
             spot = row * SIDE + ahead
             for f in range(AXES):
                 a, b, c = p.turned(f)
-                b, c = (b + row) % SIDE, (c + ahead) % SIDE
+                b, c = mod(b + row), mod(c + ahead)
                 for k in range(SIDE):
-                    picked = pick_rows(self.held[f][b * SIDE + k], self.lists[f, b, k, c], self.sizes[f])
+                    picked = pick_rows(
+                        self.held[f][b * SIDE + k],
+                        self.lists[f, b, k, c],
+                        self.sizes[f],
+                        self.kept.at[turn, f, k],
+                    )
                     self.staged[f][spot * CORES, k] = picked[:, :BLOCK]
                     self.staged[f][spot * CORES + 1, k] = picked[:, BLOCK:]
-                for core in range(CORES):
-
-                    @pl.when(self.leaves(spot, core))
-                    def _():
-                        self.to_last(f, spot, core).start()
+            for core in range(CORES):
+
+                @pl.when(self.leaves(ahead, core))
+                def _():
+                    for f in range(AXES):
+                        self.to_last(f, row, ahead, core).start()
 
     def finish(self):
         p = self.place
@@ -166,7 +185,7 @@
             rows = pl.ds(self.starts[f], self.sizes[f])
             for row in range(SIDE):
                 for k in range(SIDE):
-                    x, y, z = natural(f, k, (b + row) % SIDE, c)
+                    x, y, z = natural(f, k, mod(b + row), c)
                     self.columns[x, y, z, p.core, rows, :] = self.staged[f][row * PLANE // SIDE + p.core, k]
 
         for f in range(AXES):
@@ -183,9 +202,12 @@
 def summed(tile_col, tiles, columns, row, swap):
     total = None
 
+    blocks = SIDE * PLANE
+    flat = columns.reshape(columns.shape[0] * PLANE, *columns.shape[4:])
+
     def column(t):
-        c = (tile_col[row, t] + SIDE * PLANE) % (SIDE * PLANE + 8)
-        return columns[c // PLANE, (c // 8) % SIDE, (c // CORES) % SIDE, c % CORES]
+        c = tile_col[row, t]
+        return flat[jnp.where(c < 8, c + blocks, c - 8)]
 
     for pair in range(tiles.shape[1] // 2):
         rows = jnp.concatenate([column(2 * pair), column(2 * pair + 1)], axis=1)
@@ -213,6 +235,7 @@
     features, w_inner, few_sems, list_sent, list_got, held_sent, last_sent = scratch[18:25]
     sems_in = held_sent, last_sent, *scratch[25:29]
     sems_out = held_sent, last_sent, *scratch[29:33]
+    kept = scratch[33]
 
     place = Place()
     load_w = pltpu.make_async_copy(w_far, w_inner, few_sems.at[0])
@@ -231,12 +254,12 @@
         a, b, c = place.turned(f)
         for step in range(1, SIDE):
             for core in range(CORES):
-                greet(place.device(f, (a + step) % SIDE, b, c, core))
+                greet(place.device(f, mod(a + step), b, c, core))
     greet(place.device(0, *place.at, 1 - place.core))
 
     def lists_along(f, step):
         a, b, c = place.turned(f)
-        there = (a + step) % SIDE
+        there = mod(a + step)
         cut = [slice(None)] * AXES
         cut[f] = there
         return remote(
@@ -252,7 +275,7 @@
 
     def lists_across(f, step):
         a, b, c = place.turned(f)
-        there = (b + step) % SIDE
+        there = mod(b + step)
         return remote(
             halfway.at[cut_lists(f, there)],
             lists.at[f, b],
@@ -290,8 +313,8 @@
             lists_done(f, 0, halfway).wait_send()
             lists_done(f, 1, lists).wait()
 
-    inner = Exchange(place, sizes_in, held_in, lists, staged_in, columns_in, sems_in)
-    outer = Exchange(place, sizes_out, held_out, lists, staged_out, columns_out, sems_out)
+    inner = Exchange(place, sizes_in, held_in, lists, kept, staged_in, columns_in, sems_in)
+    outer = Exchange(place, sizes_out, held_out, lists, kept, staged_out, columns_out, sems_out)
 
     def keep(exchange, part, piece):
         chunk = exchange.held[0].shape[2]
@@ -407,6 +430,7 @@
             pltpu.SemaphoreType.DMA((AXES,)),
             *sems(),
             *sems(),
+            pltpu.VMEM((CHIPS, AXES, SIDE, BLOCK, 2 * BLOCK), bf16),
         ],
         compiler_params=pltpu.CompilerParams(
             collective_id=0, has_side_effects=True, vmem_limit_bytes=VMEM_LIMIT

time: 110 us -> 103 us (0.936)
  Pallas kernels: 108 us -> 101 us
    pallas_call x1, Pallas kernels: 108 us -> 101 us  [on_device(): pl.pallas_call(functools.partial(kernel, sizes_in, sizes_out), out_shape=...]
where the time goes in v5:
time: 103 us; the launch traced here: 102 us
  Pallas kernels  101 us (98%)
  local copies, waits for them, and re-layouts  1.62 us (2%)
    pallas_call x1, Pallas kernels, on_device(): pl.pallas_call(functools.partial(kernel, sizes_in, sizes_out), out_shape=...  101 us

profile of v5, /device:TPU:1, one launch (start us, length us, event | category | flops | bytes accessed | tf_op | source)
XLA Modules:
  0.0 102.4 jit_solution(15417454561006246896)
XLA Ops:
  0.0 100.8 %shard_map.91 = f32[41,1024]{1,0:T(8,128)} custom-call(bf16[602,1024]{1,0:T(8,128)(2,1)} %bitcast.7, bf16[602,256]{1,0:T(8,128)(2,1)} %refs_1_.1, f32[1,256]{1,0:T(1,128)} %bitcast.12, bf16[41,256]{1,0:T(8,128)(2,1)} %bitcast.10, f32[1,41]{1,0:T(1,128)} %bitcast.13, bf16[8,32,128,128]{3,2,1,0:T(8,128)(2,1)} %refs_5_.1, s32[8,32]{1,0:T(8,128)} %refs_6_.1, ...), custom_call_target="tpu_custom_call" | custom-call | tf_op jit(solution)/shard_map/pallas_call | solution.py:398
  100.8 1.6 %copy.11 = f32[1024,41]{0,1:T(8,128)} copy(f32[1024,41]{0,1:T(8,128)} %bitcast.8) | data formatting | bytes 335872
